TPU v7x, 256 devices: a whole 4x4x8 slice. The times are simulated.
256 devices in a mesh: ctx: 32 (over x, z), pb: 2 (over core), ga: 4 (over y).
Axes of the slice: x: 4, y: 4, z: 8, core: 2. Of those that a mesh axis runs over, the one named last changes fastest.
Arguments:
- queries: bfloat16 [8192, 12288], P(('ctx', 'pb'), 'ga'), may hold values from -128 to 128
- stretch_keys: bfloat16 [8192, 768], P(('ctx', 'pb'), 'ga'), may hold values from -16 to 16
- stretch_values: bfloat16 [8192, 512], P(('ctx', 'pb'), 'ga'), may hold values from -6 to 6
- prior_cache_keys: bfloat16 [131072, 768], P('ctx', 'ga'), may hold values from -16 to 16
- cache_values: bfloat16 [131072, 512], P('ctx', 'ga'), may hold values from -6 to 6
- block_lengths: int32 [32, 256], P('ctx'), may hold values from 1 to 32, 4096 in all within a row
- compress_weights: float32 [4, 32], P('ga'), may hold values from 0.1 to 1.9
- selections: int32 [128, 4, 13], P(('ctx', 'pb'), 'ga'), may hold values from 1 to 2045, as said below
- gate_logits: float32 [3, 8192, 64], P(None, ('ctx', 'pb'), 'ga'), may hold values from -6 to 6
Outputs:
- attended: bfloat16 [8192, 8192], P(('ctx', 'pb'), 'ga')
Inputs may be any that keep to these rules, and one draw needn't show every extreme that they name: `block_lengths`: each row belongs to one cache shard and sums to 4096; its largest entry is 32. `selections`: each row lists 13 different blocks, never the first or one of the last two blocks of a cache shard (a shard holds 64 blocks). Over the 2 rows of one device and one group at most 2 listed blocks lie in one cache shard, and for each group one cache shard holds exactly 2 of every device's listed blocks.
All inputs are finite; a program needn't handle non-finite values.
Results may differ from a plain program's by a relative error of at most 0.011.
Values may be sent and summed in bfloat16 or wider, within the bound.
A program may use at most 128 MiB of HBM per device.

v0:
```python
import math

import jax
import jax.numpy as jnp
from jax import lax
from jax.sharding import PartitionSpec as P

SBLK = 64
WINDOW = 512


floor_score = -1e30


def passed_along(value, axis, steps):
    count = lax.axis_size(axis)
    first, last = (max(0, -steps), min(count, count - steps))
    return lax.ppermute(value, axis, [(source, source + steps) for source in range(first, last)])


def compress_rows(cache_rows, value_rows, lengths, branch_weights):
    span = cache_rows.shape[0]
    starts = jnp.cumsum(lengths) - lengths
    positions = jnp.arange(span, dtype=jnp.int32)
    group_member = (positions[None, :] >= starts[:, None]) & (
        positions[None, :] < (starts + lengths)[:, None]
    )
    offsets = jnp.sum(jnp.where(group_member, positions[None, :] - starts[:, None], 0), axis=0)
    lookup = jnp.arange(branch_weights.shape[0], dtype=jnp.int32)
    token_weight = jnp.sum(
        jnp.where(offsets[:, None] == lookup[None, :], branch_weights[None, :], 0.0), axis=1
    )
    spread = 1.0 / jnp.sqrt(lengths.astype(jnp.float32))
    matrix = jnp.where(group_member, token_weight[None, :] * spread[:, None], 0.0).astype(
        jnp.bfloat16
    )
    packed_keys = jnp.dot(matrix, cache_rows, preferred_element_type=jnp.float32).astype(
        jnp.bfloat16
    )
    packed_values = jnp.dot(matrix, value_rows, preferred_element_type=jnp.float32).astype(
        jnp.bfloat16
    )
    return (packed_keys, packed_values)


def wanted_blocks(listed_ids, block_total):
    flat_ids = listed_ids.reshape(-1)
    always_on = jnp.array([0, block_total - 2, block_total - 1], dtype=jnp.int32)
    flat_ids = jnp.concatenate([always_on, flat_ids])
    return flat_ids


def slot_table(flat_ids, per_shard, slot_width):
    owners = flat_ids // per_shard
    position = jnp.arange(flat_ids.shape[0], dtype=jnp.int32)
    before = (owners[None, :] == owners[:, None]) & (position[None, :] < position[:, None])
    rank_count = jnp.sum(before.astype(jnp.int32), axis=1)
    return (owners * slot_width + rank_count, flat_ids % per_shard)


def asked_table(slots, offsets, shards, slot_width):
    places = jnp.arange(shards * slot_width, dtype=jnp.int32)
    matches = slots[:, None] == places[None, :]
    full_table = jnp.sum(jnp.where(matches, offsets[:, None], 0), axis=0)
    return full_table.reshape(shards, slot_width)


def on_device(
    queries,
    stretch_keys,
    stretch_values,
    prior_cache_keys,
    cache_values,
    block_lengths,
    compress_weights,
    selections,
    gate_logits,
):
    query_count = queries.shape[0]
    head_count = gate_logits.shape[2]
    key_width = prior_cache_keys.shape[1]
    value_width = cache_values.shape[1]
    score_scale = 1.0 / math.sqrt(key_width)
    query_rows = queries.reshape(query_count * head_count, key_width)
    row_count = query_rows.shape[0]
    shards = lax.axis_size("ctx")
    packed_keys, packed_values = compress_rows(
        prior_cache_keys, cache_values, block_lengths[0], compress_weights[0]
    )
    start_state = (
        jnp.full((row_count,), floor_score, jnp.float32),
        jnp.zeros((row_count,), jnp.float32),
        jnp.zeros((row_count, value_width), jnp.float32),
    )
    piece_keys = lax.all_gather(packed_keys, "ctx", axis=0, tiled=True)
    piece_values = lax.all_gather(packed_values, "ctx", axis=0, tiled=True)
    length = piece_keys.shape[0]
    stride = math.gcd(length, 1024)
    key_block = piece_keys.reshape(length // stride, stride, key_width)
    value_block = piece_values.reshape(length // stride, stride, value_width)

    def absorb(carry_state, operand):
        row_peak, running_total, blended = carry_state
        some_keys, some_values = operand
        scores = (
            lax.dot_general(
                query_rows, some_keys, (((1,), (1,)), ((), ())), preferred_element_type=jnp.float32
            )
            * score_scale
        )
        new_peak = jnp.maximum(row_peak, jnp.max(scores, axis=1))
        factor = jnp.exp(row_peak - new_peak)
        branch_weights = jnp.exp(scores - new_peak[:, None])
        running_total = running_total * factor + jnp.sum(branch_weights, axis=1)
        blended = blended * factor[:, None] + jnp.dot(
            branch_weights.astype(jnp.bfloat16), some_values, preferred_element_type=jnp.float32
        )
        return ((new_peak, running_total, blended), None)

    row_peak, running_total, blended = lax.scan(absorb, start_state, (key_block, value_block))[0]
    compressed_out = (blended / running_total[:, None]).reshape(
        query_count, head_count, value_width
    )
    listed_ids = selections[:, 0, :]
    query_blocks, listed = listed_ids.shape
    per_shard = prior_cache_keys.shape[0] // SBLK
    block_total = per_shard * shards
    slot_bound = max(2, (query_blocks * listed + shards - 1) // shards)
    key_blocks = prior_cache_keys.reshape(per_shard, SBLK, key_width)
    value_blocks = cache_values.reshape(per_shard, SBLK, value_width)
    slot_width = slot_bound + 2
    slots, offsets = slot_table(wanted_blocks(listed_ids, block_total), per_shard, slot_width)
    asked_here = asked_table(slots, offsets, shards, slot_width)
    asked_for = lax.all_to_all(asked_here, "ctx", split_axis=0, concat_axis=0, tiled=True)
    item_count = asked_for.shape[1]
    flat_asked = asked_for.reshape(-1)
    sent_keys = jnp.take(key_blocks, flat_asked, axis=0).reshape(
        shards, item_count, SBLK, key_width
    )
    sent_values = jnp.take(value_blocks, flat_asked, axis=0).reshape(
        shards, item_count, SBLK, value_width
    )
    got_keys = lax.all_to_all(sent_keys, "ctx", split_axis=0, concat_axis=0, tiled=True)
    got_values = lax.all_to_all(sent_values, "ctx", split_axis=0, concat_axis=0, tiled=True)
    picked_keys = jnp.take(got_keys.reshape(shards * slot_width, SBLK, key_width), slots, axis=0)
    picked_values = jnp.take(
        got_values.reshape(shards * slot_width, SBLK, value_width), slots, axis=0
    )
    fixed_keys = picked_keys[:3]
    fixed_values = picked_values[:3]
    listed_keys = picked_keys[3:]
    listed_values = picked_values[3:]
    selected_keys = jnp.concatenate(
        [
            jnp.broadcast_to(fixed_keys[None], (query_blocks, 3, SBLK, key_width)),
            listed_keys.reshape(query_blocks, listed, SBLK, key_width),
        ],
        axis=1,
    ).reshape(query_blocks, (3 + listed) * SBLK, key_width)
    chosen_values = jnp.concatenate(
        [
            jnp.broadcast_to(fixed_values[None], (query_blocks, 3, SBLK, value_width)),
            listed_values.reshape(query_blocks, listed, SBLK, value_width),
        ],
        axis=1,
    ).reshape(query_blocks, (3 + listed) * SBLK, value_width)
    grouped_rows = queries.reshape(query_blocks, query_count // query_blocks, head_count, key_width)
    scores = (
        jnp.einsum(
            "rjve,rse->rjvs", grouped_rows, selected_keys, preferred_element_type=jnp.float32
        )
        * score_scale
    )
    row_peak = jnp.max(scores, axis=3, keepdims=True)
    branch_weights = jnp.exp(scores - row_peak)
    row_total = jnp.sum(branch_weights, axis=3, keepdims=True)
    selected_out = (
        jnp.einsum(
            "bqhk,bkv->bqhv",
            branch_weights.astype(jnp.bfloat16),
            chosen_values,
            preferred_element_type=jnp.float32,
        )
        / row_total
    )
    selected_out = selected_out.reshape(query_count, head_count, value_width)
    reach_count = max(1, WINDOW // query_count)
    earlier_keys = []
    earlier_values = []
    for distance in range(reach_count, 0, -1):
        moved_keys, moved_values = passed_along(
            (stretch_keys, stretch_values), ("ctx", "pb"), distance
        )
        earlier_keys.append(moved_keys)
        earlier_values.append(moved_values)
    window_rows = jnp.concatenate(earlier_keys + [stretch_keys], axis=0)
    window_values = jnp.concatenate(earlier_values + [stretch_values], axis=0)
    first_query = lax.axis_index(("ctx", "pb")) * query_count
    query_pos = first_query + jnp.arange(query_count, dtype=jnp.int32)
    key_pos = (
        first_query - reach_count * query_count + jnp.arange(window_rows.shape[0], dtype=jnp.int32)
    )
    distance_grid = query_pos[:, None] - key_pos[None, :]
    allowed = (distance_grid >= 0) & (distance_grid < WINDOW) & (key_pos[None, :] >= 0)
    near_scores = (
        jnp.einsum(
            "qhd,kd->qhk",
            queries.reshape(query_count, head_count, key_width),
            window_rows,
            preferred_element_type=jnp.float32,
        )
        * score_scale
    )
    near_scores = jnp.where(allowed[:, None, :], near_scores, floor_score)
    near_peak = jnp.max(near_scores, axis=2, keepdims=True)
    near_weights = jnp.exp(near_scores - near_peak)
    near_total = jnp.sum(near_weights, axis=2, keepdims=True)
    windowed_out = (
        jnp.einsum(
            "qhk,kv->qhv",
            near_weights.astype(jnp.bfloat16),
            window_values,
            preferred_element_type=jnp.float32,
        )
        / near_total
    )
    gate_values = jax.nn.sigmoid(gate_logits)
    attended = (
        gate_values[0][..., None] * compressed_out
        + gate_values[1][..., None] * selected_out
        + gate_values[2][..., None] * windowed_out
    )
    return attended.reshape(query_count, head_count * value_width).astype(jnp.bfloat16)


def solution(mesh):
    placed = (
        P(("ctx", "pb"), "ga"),
        P(("ctx", "pb"), "ga"),
        P(("ctx", "pb"), "ga"),
        P("ctx", "ga"),
        P("ctx", "ga"),
        P("ctx", None),
        P("ga", None),
        P(("ctx", "pb"), "ga", None),
        P(None, ("ctx", "pb"), "ga"),
    )
    return jax.shard_map(
        on_device, mesh=mesh, in_specs=placed, out_specs=P(("ctx", "pb"), "ga"), check_vma=False
    )
```

profile of v0, /device:TPU:1, one launch (start us, length us, event | category | flops | bytes accessed | tf_op | source)
XLA Modules:
  0.0 362.0 jit_solution(14902906855570495999)
XLA Ops:
  17.9 11.9 %all-to-all-start = ((s32[32,1,4]{2,1,0:T(1,128)}), s32[32,1,4]{2,1,0:T(1,128)S(1)}, u32[]{:S(2)}, u32[]{:S(2)}) async-start(s32[32,1,4]{2,1,0:T(1,128)} %bitcast.9), calls=%async_computation | async-start | bytes 32768 | tf_op jit(solution)/shard_map/all_to_all | solution.py:134
  29.7 4.0 %collective-permute-start = (bf16[128,192]{0,1:T(8,128)(2,1)S(1)}, bf16[128,192]{0,1:T(8,128)(2,1)S(1)}, u32[]{:S(2)}, u32[]{:S(2)}) collective-permute-start(bf16[128,192]{0,1:T(8,128)(2,1)S(1)} %copy-done.8), channel_id=1, source_target_pairs={{0,16},{4,20},{8,24},{12,28},{16,32},{20,36},{24,40},{28,44},{32,4... | collective-permute-start | bytes 147464 | tf_op jit(solution)/shard_map/ppermute | solution.py:18
  33.8 6.6 %collective-permute-start.1 = (bf16[128,192]{0,1:T(8,128)(2,1)S(1)}, bf16[128,192]{0,1:T(8,128)(2,1)S(1)}, u32[]{:S(2)}, u32[]{:S(2)}) collective-permute-start(bf16[128,192]{0,1:T(8,128)(2,1)S(1)} %copy-done.8), channel_id=1, source_target_pairs={{0,12},{4,16},{8,20},{12,24},{16,28},{20,32},{24,36},{28,40},{32,4... | collective-permute-start | bytes 147464 | tf_op jit(solution)/shard_map/ppermute | solution.py:18
  50.8 8.8 %all-to-all-start.2 = ((bf16[32,4,64,128]{3,2,1,0:T(8,128)(2,1)}), bf16[32,4,64,128]{3,2,1,0:T(8,128)(2,1)}, u32[]{:S(2)}, u32[]{:S(2)}) async-start(bf16[32,4,64,128]{3,2,1,0:T(8,128)(2,1)} %broadcast_select_fusion.1), calls=%async_computation.2 | async-start | bytes 4194304 | tf_op jit(solution)/shard_map/all_to_all | solution.py:144
  61.6 3.9 %copy.85 = bf16[4096,192]{1,0:T(8,128)(2,1)} copy(bf16[4096,192]{0,1:T(8,128)(2,1)} %param.15) | data formatting | bytes 3145728 | tf_op args[3]
  71.0 4.5 %gather_fusion = bf16[128,64,192]{2,1,0:T(8,128)(2,1)} fusion(bf16[64,64,192]{2,1,0:T(8,128)(2,1)} %bitcast.102, s32[1024]{0:T(1024)} %copy-done.15), kind=kCustom, calls=%fused_computation | custom fusion | bytes 6291968 | tf_op jit(solution)/shard_map/jit(_take)/gather | solution.py:137
  75.5 4.6 %broadcast_select_fusion = bf16[32,4,64,192]{3,2,1,0:T(8,128)(2,1)} fusion(bf16[32,4,64,192]{3,2,1,0:T(8,128)(2,1)} %bitcast.103, pred[32,4]{1,0:T(8,128)(4,1)S(1)} %copy.84), kind=kLoop, calls=%fused_computation.42 | loop fusion | flops 1572864 | bytes 6291584 | tf_op jit(solution)/shard_map/jit(_take)/select_n | solution.py:137
  80.2 5.2 %collective-permute-start.5 = (bf16[128,128]{0,1:T(8,128)(2,1)S(1)}, bf16[128,128]{0,1:T(8,128)(2,1)S(1)}, u32[]{:S(2)}, u32[]{:S(2)}) collective-permute-start(bf16[128,128]{0,1:T(8,128)(2,1)S(1)} %copy.92), channel_id=1, source_target_pairs={{0,12},{4,16},{8,20},{12,24},{16,28},{20,32},{24,36},{28,40},{32,4... | collective-permute-start | bytes 98312 | tf_op jit(solution)/shard_map/ppermute | solution.py:18
  85.4 25.0 %collective-permute-done.5 = bf16[128,128]{0,1:T(8,128)(2,1)S(1)} collective-permute-done((bf16[128,128]{0,1:T(8,128)(2,1)S(1)}, bf16[128,128]{0,1:T(8,128)(2,1)S(1)}, u32[]{:S(2)}, u32[]{:S(2)}) %collective-permute-start.5) | collective-permute-done | bytes 32800 | tf_op jit(solution)/shard_map/ppermute | solution.py:18
  110.4 9.0 %collective-permute-start.6 = (bf16[128,128]{0,1:T(8,128)(2,1)S(1)}, bf16[128,128]{0,1:T(8,128)(2,1)S(1)}, u32[]{:S(2)}, u32[]{:S(2)}) collective-permute-start(bf16[128,128]{0,1:T(8,128)(2,1)S(1)} %copy.92), channel_id=1, source_target_pairs={{0,8},{4,12},{8,16},{12,20},{16,24},{20,28},{24,32},{28,36},{32,40... | collective-permute-start | bytes 98312 | tf_op jit(solution)/shard_map/ppermute | solution.py:18
  120.4 5.9 %collective-permute-start.7 = (bf16[128,128]{0,1:T(8,128)(2,1)S(1)}, bf16[128,128]{0,1:T(8,128)(2,1)S(1)}, u32[]{:S(2)}, u32[]{:S(2)}) collective-permute-start(bf16[128,128]{0,1:T(8,128)(2,1)S(1)} %copy.92), channel_id=1, source_target_pairs={{0,4},{4,8},{8,12},{12,16},{16,20},{20,24},{24,28},{28,32},{32,36}... | collective-permute-start | bytes 98312 | tf_op jit(solution)/shard_map/ppermute | solution.py:18
  132.5 10.7 %all-to-all-start.1 = ((bf16[32,4,64,192]{3,2,1,0:T(8,128)(2,1)}), bf16[32,4,64,192]{3,2,1,0:T(8,128)(2,1)}, u32[]{:S(2)}, u32[]{:S(2)}) async-start(bf16[32,4,64,192]{3,2,1,0:T(8,128)(2,1)} %broadcast_select_fusion), calls=%async_computation.1 | async-start | bytes 8388608 | tf_op jit(solution)/shard_map/all_to_all | solution.py:143
  146.5 6.0 %copy.102 = bf16[8192,192]{1,0:T(8,128)(2,1)} copy(bf16[8192,192]{0,1:T(8,128)(2,1)} %all-gather.3.cloned.1.call-done) | data formatting | bytes 6291456
  152.5 70.4 %all-gather.5.cloned.1.call-done = bf16[8192,128]{1,0:T(8,128)(2,1)} async-done(((bf16[256,128]{1,0:T(8,128)(2,1)}), bf16[8192,128]{1,0:T(8,128)(2,1)}) %all-gather.5.cloned.1.call-update) | async-done | bytes 2097168 | tf_op jit(solution)/shard_map/all_gather | solution.py:96
  222.8 114.3 %while.15 = (s32[]{:T(128)}, f32[2048]{0:T(1024)S(1)}, f32[2048]{0:T(1024)S(1)}, f32[2048,128]{1,0:T(8,128)S(1)}, bf16[8,1024,192]{2,1,0:T(8,128)(2,1)}, /*index...) while((s32[]{:T(128)}, f32[2048]{0:T(1024)S(1)}, ...), condition=%wide.region_7.8_spmd.clone, body=%wide.region_4.7_spmd.clone.sunk | while | flops 1359751168 | bytes 62522500 | solution.py:120
  222.8 5.5 %multiply_reduce_fusion.2 = (f32[2048]{0:T(1024)S(1)}, f32[1024,2048]{1,0:T(8,128)}) fusion(bf16[2048,192]{1,0:T(8,128)(2,1)S(1)} %get-tuple-element.209, bf16[8,1024,192]{2,1,0:T(8,128)(2,1)} %get-tuple-element.208, s32[]{:T(128)} %get-tuple-element.195), kind=kOutput, calls=%fused_computation.5.clone.1 | convolution fusion | flops 809498624 | bytes 9708032 | tf_op jit(solution)/shard_map/while/body/eval_jaxpr/dot_general | solution.py:106
  228.4 4.9 %fusion.72 = f32[2048]{0:T(1024)S(1)} fusion(f32[1024,2048]{1,0:T(8,128)} %get-tuple-element.183, f32[2048]{0:T(1024)S(1)} %select_maximum_fusion.2), kind=kLoop, calls=%fused_computation.7.clone.1 | loop fusion | flops 6289408 | bytes 8404992 | tf_op jit(solution)/shard_map/while/body/eval_jaxpr/reduce_sum | solution.py:114
  237.1 5.6 %multiply_reduce_fusion.2 = (f32[2048]{0:T(1024)S(1)}, f32[1024,2048]{1,0:T(8,128)}) fusion(bf16[2048,192]{1,0:T(8,128)(2,1)S(1)} %get-tuple-element.209, bf16[8,1024,192]{2,1,0:T(8,128)(2,1)} %get-tuple-element.208, s32[]{:T(128)} %get-tuple-element.195), kind=kOutput, calls=%fused_computation.5.clone.1 | convolution fusion | flops 809498624 | bytes 9708032 | tf_op jit(solution)/shard_map/while/body/eval_jaxpr/dot_general | solution.py:106
  242.7 4.9 %fusion.72 = f32[2048]{0:T(1024)S(1)} fusion(f32[1024,2048]{1,0:T(8,128)} %get-tuple-element.183, f32[2048]{0:T(1024)S(1)} %select_maximum_fusion.2), kind=kLoop, calls=%fused_computation.7.clone.1 | loop fusion | flops 6289408 | bytes 8404992 | tf_op jit(solution)/shard_map/while/body/eval_jaxpr/reduce_sum | solution.py:114
  251.4 5.6 %multiply_reduce_fusion.2 = (f32[2048]{0:T(1024)S(1)}, f32[1024,2048]{1,0:T(8,128)}) fusion(bf16[2048,192]{1,0:T(8,128)(2,1)S(1)} %get-tuple-element.209, bf16[8,1024,192]{2,1,0:T(8,128)(2,1)} %get-tuple-element.208, s32[]{:T(128)} %get-tuple-element.195), kind=kOutput, calls=%fused_computation.5.clone.1 | convolution fusion | flops 809498624 | bytes 9708032 | tf_op jit(solution)/shard_map/while/body/eval_jaxpr/dot_general | solution.py:106
  257.0 4.9 %fusion.72 = f32[2048]{0:T(1024)S(1)} fusion(f32[1024,2048]{1,0:T(8,128)} %get-tuple-element.183, f32[2048]{0:T(1024)S(1)} %select_maximum_fusion.2), kind=kLoop, calls=%fused_computation.7.clone.1 | loop fusion | flops 6289408 | bytes 8404992 | tf_op jit(solution)/shard_map/while/body/eval_jaxpr/reduce_sum | solution.py:114
  265.7 5.6 %multiply_reduce_fusion.2 = (f32[2048]{0:T(1024)S(1)}, f32[1024,2048]{1,0:T(8,128)}) fusion(bf16[2048,192]{1,0:T(8,128)(2,1)S(1)} %get-tuple-element.209, bf16[8,1024,192]{2,1,0:T(8,128)(2,1)} %get-tuple-element.208, s32[]{:T(128)} %get-tuple-element.195), kind=kOutput, calls=%fused_computation.5.clone.1 | convolution fusion | flops 809498624 | bytes 9708032 | tf_op jit(solution)/shard_map/while/body/eval_jaxpr/dot_general | solution.py:106
  271.3 4.9 %fusion.72 = f32[2048]{0:T(1024)S(1)} fusion(f32[1024,2048]{1,0:T(8,128)} %get-tuple-element.183, f32[2048]{0:T(1024)S(1)} %select_maximum_fusion.2), kind=kLoop, calls=%fused_computation.7.clone.1 | loop fusion | flops 6289408 | bytes 8404992 | tf_op jit(solution)/shard_map/while/body/eval_jaxpr/reduce_sum | solution.py:114
  280.0 5.6 %multiply_reduce_fusion.2 = (f32[2048]{0:T(1024)S(1)}, f32[1024,2048]{1,0:T(8,128)}) fusion(bf16[2048,192]{1,0:T(8,128)(2,1)S(1)} %get-tuple-element.209, bf16[8,1024,192]{2,1,0:T(8,128)(2,1)} %get-tuple-element.208, s32[]{:T(128)} %get-tuple-element.195), kind=kOutput, calls=%fused_computation.5.clone.1 | convolution fusion | flops 809498624 | bytes 9708032 | tf_op jit(solution)/shard_map/while/body/eval_jaxpr/dot_general | solution.py:106
  285.5 4.9 %fusion.72 = f32[2048]{0:T(1024)S(1)} fusion(f32[1024,2048]{1,0:T(8,128)} %get-tuple-element.183, f32[2048]{0:T(1024)S(1)} %select_maximum_fusion.2), kind=kLoop, calls=%fused_computation.7.clone.1 | loop fusion | flops 6289408 | bytes 8404992 | tf_op jit(solution)/shard_map/while/body/eval_jaxpr/reduce_sum | solution.py:114
  294.3 5.6 %multiply_reduce_fusion.2 = (f32[2048]{0:T(1024)S(1)}, f32[1024,2048]{1,0:T(8,128)}) fusion(bf16[2048,192]{1,0:T(8,128)(2,1)S(1)} %get-tuple-element.209, bf16[8,1024,192]{2,1,0:T(8,128)(2,1)} %get-tuple-element.208, s32[]{:T(128)} %get-tuple-element.195), kind=kOutput, calls=%fused_computation.5.clone.1 | convolution fusion | flops 809498624 | bytes 9708032 | tf_op jit(solution)/shard_map/while/body/eval_jaxpr/dot_general | solution.py:106
  299.8 4.9 %fusion.72 = f32[2048]{0:T(1024)S(1)} fusion(f32[1024,2048]{1,0:T(8,128)} %get-tuple-element.183, f32[2048]{0:T(1024)S(1)} %select_maximum_fusion.2), kind=kLoop, calls=%fused_computation.7.clone.1 | loop fusion | flops 6289408 | bytes 8404992 | tf_op jit(solution)/shard_map/while/body/eval_jaxpr/reduce_sum | solution.py:114
  308.6 5.6 %multiply_reduce_fusion.2 = (f32[2048]{0:T(1024)S(1)}, f32[1024,2048]{1,0:T(8,128)}) fusion(bf16[2048,192]{1,0:T(8,128)(2,1)S(1)} %get-tuple-element.209, bf16[8,1024,192]{2,1,0:T(8,128)(2,1)} %get-tuple-element.208, s32[]{:T(128)} %get-tuple-element.195), kind=kOutput, calls=%fused_computation.5.clone.1 | convolution fusion | flops 809498624 | bytes 9708032 | tf_op jit(solution)/shard_map/while/body/eval_jaxpr/dot_general | solution.py:106
  314.1 4.9 %fusion.72 = f32[2048]{0:T(1024)S(1)} fusion(f32[1024,2048]{1,0:T(8,128)} %get-tuple-element.183, f32[2048]{0:T(1024)S(1)} %select_maximum_fusion.2), kind=kLoop, calls=%fused_computation.7.clone.1 | loop fusion | flops 6289408 | bytes 8404992 | tf_op jit(solution)/shard_map/while/body/eval_jaxpr/reduce_sum | solution.py:114
  322.9 5.6 %multiply_reduce_fusion.2 = (f32[2048]{0:T(1024)S(1)}, f32[1024,2048]{1,0:T(8,128)}) fusion(bf16[2048,192]{1,0:T(8,128)(2,1)S(1)} %get-tuple-element.209, bf16[8,1024,192]{2,1,0:T(8,128)(2,1)} %get-tuple-element.208, s32[]{:T(128)} %get-tuple-element.195), kind=kOutput, calls=%fused_computation.5.clone.1 | convolution fusion | flops 809498624 | bytes 9708032 | tf_op jit(solution)/shard_map/while/body/eval_jaxpr/dot_general | solution.py:106
  328.4 4.9 %fusion.72 = f32[2048]{0:T(1024)S(1)} fusion(f32[1024,2048]{1,0:T(8,128)} %get-tuple-element.183, f32[2048]{0:T(1024)S(1)} %select_maximum_fusion.2), kind=kLoop, calls=%fused_computation.7.clone.1 | loop fusion | flops 6289408 | bytes 8404992 | tf_op jit(solution)/shard_map/while/body/eval_jaxpr/reduce_sum | solution.py:114
  348.2 4.9 %add_convert_fusion = bf16[128,16,128]{0,2,1:T(8,128)(2,1)} fusion(f32[128,16,128]{0,2,1:T(8,128)S(1)} %copy.90, f32[128,16,128]{0,2,1:T(8,128)S(1)} %copy.81, f32[640,128,16]{1,0,2:T(8,128)} %copy-done.5, f32[128,16]{0,1:T(8,128)S(1)} %get-tuple-element.133, pred[128,640]{0,1:T(8,128)(4,1)S(1)} %fusion.44, f32[128,16]{0,1:T(8,128)S(1)} %fusion.21, ...), kind=kOutput, calls=%fused_computation.54 | convolution fusion | flops 342622208 | bytes 8151040 | tf_op jit(solution)/shard_map/qhk,kv->qhv/dot_general | solution.py:219
  (180 shorter events, 82.3 us)
Async XLA Ops:
  6.5 41.7 %copy-start = (bf16[4096,128]{1,0:T(8,128)(2,1)S(1)}, bf16[4096,128]{1,0:T(8,128)(2,1)}, u32[]{:S(2)}) copy-start(bf16[4096,128]{1,0:T(8,128)(2,1)} %param.16) | copy-start | bytes 3145732
  6.5 140.0 %all-gather.3.cloned.1.call-start = ((), (), s32[]{:S(2)}) async-start(), calls=%async_computation.3 | async-start | bytes 3244032 | tf_op jit(solution)/shard_map/all_gather | solution.py:95
  11.5 4.0 %copy-start.17 = (s32[2,1,13]{2,1,0:T(1,128)S(1)}, s32[2,1,13]{2,1,0:T(1,128)}, u32[]{:S(2)}) copy-start(s32[2,1,13]{2,1,0:T(1,128)} %param.19) | copy-start | bytes 316
  11.5 4.8 %copy-start.19 = (s32[3]{0:T(128)S(1)}, s32[3]{0:T(128)}, u32[]{:S(2)}) copy-start(s32[3]{0:T(128)} %constant.139.clone) | copy-start | bytes 40
  11.5 18.2 %copy-start.8 = (bf16[128,192]{0,1:T(8,128)(2,1)S(1)}, bf16[128,192]{0,1:T(8,128)(2,1)}, u32[]{:S(2)}) copy-start(bf16[128,192]{0,1:T(8,128)(2,1)} %param.13) | copy-start | bytes 147460
  11.5 33.3 %copy-start.9 = (bf16[128,128]{1,0:T(8,128)(2,1)S(1)}, bf16[128,128]{1,0:T(8,128)(2,1)}, u32[]{:S(2)}) copy-start(bf16[128,128]{1,0:T(8,128)(2,1)} %param.14) | copy-start | bytes 98308
  17.9 29.3 %all-to-all-start = ((s32[32,1,4]{2,1,0:T(1,128)}), s32[32,1,4]{2,1,0:T(1,128)S(1)}, u32[]{:S(2)}, u32[]{:S(2)}) async-start(s32[32,1,4]{2,1,0:T(1,128)} %bitcast.9), calls=%async_computation | async-start | bytes 32768 | tf_op jit(solution)/shard_map/all_to_all | solution.py:134
  29.7 98.1 %collective-permute-start = (bf16[128,192]{0,1:T(8,128)(2,1)S(1)}, bf16[128,192]{0,1:T(8,128)(2,1)S(1)}, u32[]{:S(2)}, u32[]{:S(2)}) collective-permute-start(bf16[128,192]{0,1:T(8,128)(2,1)S(1)} %copy-done.8), channel_id=1, source_target_pairs={{0,16},{4,20},{8,24},{12,28},{16,32},{20,36},{24,40},{28,44},{32,4... | collective-permute-start | bytes 147464 | tf_op jit(solution)/shard_map/ppermute | solution.py:18
  33.8 94.1 %collective-permute-start.1 = (bf16[128,192]{0,1:T(8,128)(2,1)S(1)}, bf16[128,192]{0,1:T(8,128)(2,1)S(1)}, u32[]{:S(2)}, u32[]{:S(2)}) collective-permute-start(bf16[128,192]{0,1:T(8,128)(2,1)S(1)} %copy-done.8), channel_id=1, source_target_pairs={{0,12},{4,16},{8,20},{12,24},{16,28},{20,32},{24,36},{28,40},{32,4... | collective-permute-start | bytes 147464 | tf_op jit(solution)/shard_map/ppermute | solution.py:18
  40.4 87.5 %collective-permute-start.2 = (bf16[128,192]{0,1:T(8,128)(2,1)S(1)}, bf16[128,192]{0,1:T(8,128)(2,1)S(1)}, u32[]{:S(2)}, u32[]{:S(2)}) collective-permute-start(bf16[128,192]{0,1:T(8,128)(2,1)S(1)} %copy-done.8), channel_id=1, source_target_pairs={{0,8},{4,12},{8,16},{12,20},{16,24},{20,28},{24,32},{28,36},{32,40... | collective-permute-start | bytes 147464 | tf_op jit(solution)/shard_map/ppermute | solution.py:18
  42.6 85.4 %collective-permute-start.3 = (bf16[128,192]{0,1:T(8,128)(2,1)S(1)}, bf16[128,192]{0,1:T(8,128)(2,1)S(1)}, u32[]{:S(2)}, u32[]{:S(2)}) collective-permute-start(bf16[128,192]{0,1:T(8,128)(2,1)S(1)} %copy-done.8), channel_id=1, source_target_pairs={{0,4},{4,8},{8,12},{12,16},{16,20},{20,24},{24,28},{28,32},{32,36}... | collective-permute-start | bytes 147464 | tf_op jit(solution)/shard_map/ppermute | solution.py:18
  44.9 35.2 %collective-permute-start.4 = (bf16[128,128]{0,1:T(8,128)(2,1)S(1)}, bf16[128,128]{0,1:T(8,128)(2,1)S(1)}, u32[]{:S(2)}, u32[]{:S(2)}) collective-permute-start(bf16[128,128]{0,1:T(8,128)(2,1)S(1)} %copy.92), channel_id=1, source_target_pairs={{0,16},{4,20},{8,24},{12,28},{16,32},{20,36},{24,40},{28,44},{32,4... | collective-permute-start | bytes 98312 | tf_op jit(solution)/shard_map/ppermute | solution.py:18
  50.8 81.6 %all-to-all-start.2 = ((bf16[32,4,64,128]{3,2,1,0:T(8,128)(2,1)}), bf16[32,4,64,128]{3,2,1,0:T(8,128)(2,1)}, u32[]{:S(2)}, u32[]{:S(2)}) async-start(bf16[32,4,64,128]{3,2,1,0:T(8,128)(2,1)} %broadcast_select_fusion.1), calls=%async_computation.2 | async-start | bytes 4194304 | tf_op jit(solution)/shard_map/all_to_all | solution.py:144
  59.6 5.9 %copy-start.3 = (bf16[128,3072]{1,0:T(8,128)(2,1)S(1)}, bf16[128,3072]{1,0:T(8,128)(2,1)}, u32[]{:S(2)}) copy-start(bf16[128,3072]{1,0:T(8,128)(2,1)} %param.12) | copy-start | bytes 2359300
  59.6 163.2 %all-gather.5.cloned.1.call-start = ((), (), s32[]{:S(2)}) async-start(), calls=%async_computation.4 | async-start | bytes 2162688 | tf_op jit(solution)/shard_map/all_gather | solution.py:96
  61.6 8.5 %copy-start.18 = (s32[3,1]{0,1:T(1,128)S(1)}, s32[3,1]{0,1:T(1,128)}, u32[]{:S(2)}) copy-start(s32[3,1]{0,1:T(1,128)} %constant.143) | copy-start | bytes 40
  61.6 8.6 %copy-start.10 = (f32[3,128,16]{1,2,0:T(8,128)S(1)}, f32[3,128,16]{1,2,0:T(8,128)}, u32[]{:S(2)}) copy-start(f32[3,128,16]{1,2,0:T(8,128)} %param.20) | copy-start | bytes 73732
  75.5 52.5 %copy-start.6 = (bf16[128,3072]{0,1:T(8,128)(2,1)S(1)}, bf16[128,3072]{0,1:T(8,128)(2,1)}, u32[]{:S(2)}) copy-start(bf16[128,3072]{0,1:T(8,128)(2,1)} %copy.91) | copy-start | bytes 2359300
  80.2 30.3 %collective-permute-start.5 = (bf16[128,128]{0,1:T(8,128)(2,1)S(1)}, bf16[128,128]{0,1:T(8,128)(2,1)S(1)}, u32[]{:S(2)}, u32[]{:S(2)}) collective-permute-start(bf16[128,128]{0,1:T(8,128)(2,1)S(1)} %copy.92), channel_id=1, source_target_pairs={{0,12},{4,16},{8,20},{12,24},{16,28},{20,32},{24,36},{28,40},{32,4... | collective-permute-start | bytes 98312 | tf_op jit(solution)/shard_map/ppermute | solution.py:18
  110.4 10.0 %collective-permute-start.6 = (bf16[128,128]{0,1:T(8,128)(2,1)S(1)}, bf16[128,128]{0,1:T(8,128)(2,1)S(1)}, u32[]{:S(2)}, u32[]{:S(2)}) collective-permute-start(bf16[128,128]{0,1:T(8,128)(2,1)S(1)} %copy.92), channel_id=1, source_target_pairs={{0,8},{4,12},{8,16},{12,20},{16,24},{20,28},{24,32},{28,36},{32,40... | collective-permute-start | bytes 98312 | tf_op jit(solution)/shard_map/ppermute | solution.py:18
  120.4 6.8 %collective-permute-start.7 = (bf16[128,128]{0,1:T(8,128)(2,1)S(1)}, bf16[128,128]{0,1:T(8,128)(2,1)S(1)}, u32[]{:S(2)}, u32[]{:S(2)}) collective-permute-start(bf16[128,128]{0,1:T(8,128)(2,1)S(1)} %copy.92), channel_id=1, source_target_pairs={{0,4},{4,8},{8,12},{12,16},{16,20},{20,24},{24,28},{28,32},{32,36}... | collective-permute-start | bytes 98312 | tf_op jit(solution)/shard_map/ppermute | solution.py:18
  132.4 13.0 %copy-start.16 = (pred[29]{0:T(512)(128)(4,1)S(1)}, pred[29]{0:T(512)(128)(4,1)}, u32[]{:S(2)}) copy-start(pred[29]{0:T(512)(128)(4,1)} %get-tuple-element.122) | copy-start | bytes 91
  132.5 205.5 %all-to-all-start.1 = ((bf16[32,4,64,192]{3,2,1,0:T(8,128)(2,1)}), bf16[32,4,64,192]{3,2,1,0:T(8,128)(2,1)}, u32[]{:S(2)}, u32[]{:S(2)}) async-start(bf16[32,4,64,192]{3,2,1,0:T(8,128)(2,1)} %broadcast_select_fusion), calls=%async_computation.1 | async-start | bytes 8388608 | tf_op jit(solution)/shard_map/all_to_all | solution.py:143
  228.4 5.8 %copy-start.2 = (f32[1024,2048]{1,0:T(8,128)S(1)}, f32[1024,2048]{1,0:T(8,128)}, u32[]{:S(2)}) copy-start(f32[1024,2048]{1,0:T(8,128)} %get-tuple-element.183) | copy-start | bytes 25165828 | tf_op jit(solution)/shard_map/while
  242.7 5.8 %copy-start.2 = (f32[1024,2048]{1,0:T(8,128)S(1)}, f32[1024,2048]{1,0:T(8,128)}, u32[]{:S(2)}) copy-start(f32[1024,2048]{1,0:T(8,128)} %get-tuple-element.183) | copy-start | bytes 25165828 | tf_op jit(solution)/shard_map/while
  257.0 5.8 %copy-start.2 = (f32[1024,2048]{1,0:T(8,128)S(1)}, f32[1024,2048]{1,0:T(8,128)}, u32[]{:S(2)}) copy-start(f32[1024,2048]{1,0:T(8,128)} %get-tuple-element.183) | copy-start | bytes 25165828 | tf_op jit(solution)/shard_map/while
  271.3 5.8 %copy-start.2 = (f32[1024,2048]{1,0:T(8,128)S(1)}, f32[1024,2048]{1,0:T(8,128)}, u32[]{:S(2)}) copy-start(f32[1024,2048]{1,0:T(8,128)} %get-tuple-element.183) | copy-start | bytes 25165828 | tf_op jit(solution)/shard_map/while
  285.5 5.8 %copy-start.2 = (f32[1024,2048]{1,0:T(8,128)S(1)}, f32[1024,2048]{1,0:T(8,128)}, u32[]{:S(2)}) copy-start(f32[1024,2048]{1,0:T(8,128)} %get-tuple-element.183) | copy-start | bytes 25165828 | tf_op jit(solution)/shard_map/while
  299.8 5.8 %copy-start.2 = (f32[1024,2048]{1,0:T(8,128)S(1)}, f32[1024,2048]{1,0:T(8,128)}, u32[]{:S(2)}) copy-start(f32[1024,2048]{1,0:T(8,128)} %get-tuple-element.183) | copy-start | bytes 25165828 | tf_op jit(solution)/shard_map/while
  314.1 5.8 %copy-start.2 = (f32[1024,2048]{1,0:T(8,128)S(1)}, f32[1024,2048]{1,0:T(8,128)}, u32[]{:S(2)}) copy-start(f32[1024,2048]{1,0:T(8,128)} %get-tuple-element.183) | copy-start | bytes 25165828 | tf_op jit(solution)/shard_map/while
  328.4 5.8 %copy-start.2 = (f32[1024,2048]{1,0:T(8,128)S(1)}, f32[1024,2048]{1,0:T(8,128)}, u32[]{:S(2)}) copy-start(f32[1024,2048]{1,0:T(8,128)} %get-tuple-element.183) | copy-start | bytes 25165828 | tf_op jit(solution)/shard_map/while
  348.2 7.0 %copy-start.1 = (bf16[4096,128]{1,0:T(8,128)(2,1)S(1)}, bf16[4096,128]{1,0:T(8,128)(2,1)}, u32[]{:S(2)}) copy-start(bf16[4096,128]{1,0:T(8,128)(2,1)} %param.16) | copy-start | bytes 3145732
  (8 other events, 14.2 us)
Sparse Core Ops, SparseCore 0:
  15.0 111.1 all-gather.2
  128.8 94.0 all-gather.4
where the time goes:
time: 365 us; the launch traced here: 362 us
  waiting for transfers between devices  97.2 us (27%)
  matrix products  82.9 us (23%)
  starting transfers between devices  68.8 us (19%)
  other arithmetic  57.9 us (16%)
  local copies, waits for them, and re-layouts  40.9 us (11%)
  between operations  14.1 us (4%)
    all_gather x1, waiting for transfers between devices, on_device(): piece_values = lax.all_gather(packed_values, 'ctx', axis=0, tiled=True)  70.4 us
    dot_general x8, matrix products, absorb(): lax.dot_general(query_rows, some_keys, (((1,), (1,)), ((), ())), preferre...  44.4 us
    reduce_sum x8, other arithmetic, absorb(): running_total = running_total * factor + jnp.sum(branch_weights, axis=1)  39.5 us
    ppermute x8, starting transfers between devices, passed_along(): lax.ppermute(value, axis, [(source, source + steps) for source in range(f...  37.3 us
    ppermute x8, waiting for transfers between devices, passed_along(): lax.ppermute(value, axis, [(source, source + steps) for source in range(f...  26.8 us
    dot_general x8, matrix products, absorb(): jnp.dot(branch_weights.astype(jnp.bfloat16), some_values, preferred_eleme...  23.5 us
    unnamed x51, local copies, waits for them, and re-layouts  15 us
    all_to_all x1, starting transfers between devices, on_device(): lax.all_to_all(asked_here, 'ctx', split_axis=0, concat_axis=0, tiled=True)  11.9 us
  transfers between devices with their start and end apart: 13, of which 4 were waited for; matrix products, arithmetic and copies ran while one was open for 40% of the time, Pallas kernels for 0%

commit v1 on v0

v1 whole, which is shorter than its diff:
```python
import functools
import math

import jax
import jax.numpy as jnp
from jax import lax
from jax.experimental import pallas as pl
from jax.experimental.pallas import tpu as pltpu
from jax.sharding import PartitionSpec as P

SBLK = 64
WINDOW = 512
XN, ZN = 4, 8
CN = XN * ZN
HEADS = 16
DK, DV = 192, 128
UNIT = 128
PACK = UNIT * 5 // 2
SPACK = SBLK * 5 // 2
NEAR = (0, 1, 7, 2)
FAR = (6, 3, 5, 4)
ROWS = 2048
CHUNK = 512
MESH = pl.DeviceIdType.MESH
LOW = -1e30
CEXP = math.log2(math.e) / math.sqrt(DK)
F32 = jnp.float32
BF16 = jnp.bfloat16


def pack_keys(k):
    n = k.shape[0]
    tail = k[:, 128:192]
    return k[:, :128], jnp.concatenate([tail[: n // 2], tail[n // 2 :]], axis=1)


def dot_t(a, b):
    return lax.dot_general(a, b, (((1,), (1,)), ((), ())), preferred_element_type=F32)


def body(
    asked,
    picks,
    cw,
    lengths,
    queries,
    sk,
    sv,
    ck,
    cv,
    gl,
    out,
    gat,
    send,
    recv,
    win,
    qs,
    acc,
    peak,
    mixed,
    gate,
    kt,
    vt,
    z_send,
    x_send,
    x2_send,
    d_send,
    g_recv,
    a_send,
    a_recv,
    w_send,
    w_recv,
    f_send,
    f_recv,
):
    ctx = lax.axis_index("ctx")
    p = lax.axis_index("pb")
    x = ctx // ZN
    z = lax.rem(ctx, ZN)
    flat = ctx * 2 + p
    other = 1 - p

    def at(dx, dz):
        return lax.rem(x + dx + XN, XN) * ZN + lax.rem(z + dz + ZN, ZN)

    def remote(src, dst, ssem, rsem, c, q):
        return pltpu.make_async_remote_copy(
            src_ref=src,
            dst_ref=dst,
            send_sem=ssem,
            recv_sem=rsem,
            device_id={"ctx": c, "pb": q},
            device_id_type=MESH,
        )

    barrier = pltpu.get_barrier_semaphore()

    def greet(i, carry):
        c = lax.rem(ctx + i // 2, CN)
        q = lax.rem(p + lax.rem(i, 2), 2)
        pl.semaphore_signal(barrier, inc=1, device_id={"ctx": c, "pb": q}, device_id_type=MESH)
        return carry

    lax.fori_loop(1, 2 * CN, greet, 0)

    k0, k1 = pack_keys(sk[...].astype(F32))
    win[4, 0:128, :] = k0.astype(BF16)
    win[4, 128:192, :] = k1.astype(BF16)
    win[4, 192:320, :] = sv[...]
    for k in range(1, 5):

        @pl.when(flat < k)
        def _():
            win[4 - k] = jnp.zeros((PACK, 128), BF16)

    b_at = p * UNIT + lax.broadcasted_iota(jnp.int32, (UNIT, 256), 0)
    j_at = lax.broadcasted_iota(jnp.int32, (UNIT, 256), 1)
    n_row = jnp.broadcast_to(lengths[...], (UNIT, 256)).astype(F32)
    starts = jnp.sum(jnp.where(j_at < b_at, n_row, 0.0), axis=1, keepdims=True)
    counts = jnp.sum(jnp.where(j_at == b_at, n_row, 0.0), axis=1, keepdims=True)
    spread = 1.0 / jnp.sqrt(counts)
    span = ck.shape[0] * SBLK
    step = 512
    total_k = jnp.zeros((UNIT, DK), F32)
    total_v = jnp.zeros((UNIT, DV), F32)
    for t in range(0, span, step):
        pos = (lax.broadcasted_iota(jnp.int32, (UNIT, step), 1) + t).astype(F32)
        away = pos - starts
        member = (away >= 0.0) & (away < counts)
        offs = jnp.sum(jnp.where(member, away, 0.0), axis=0, keepdims=True)
        weight = jnp.zeros((1, step), F32)
        for i in range(32):
            weight = jnp.where(offs == float(i), cw[0, i], weight)
        matrix = jnp.where(member, weight * spread, 0.0).astype(BF16)
        rows = ck[t // SBLK : (t + step) // SBLK].reshape(step, DK)
        vals = cv[t // SBLK : (t + step) // SBLK].reshape(step, DV)
        total_k += jnp.dot(matrix, rows, preferred_element_type=F32)
        total_v += jnp.dot(matrix, vals, preferred_element_type=F32)
    k0, k1 = pack_keys(total_k)
    gat[0, 0, p, 0:128, :] = k0.astype(BF16)
    gat[0, 0, p, 128:192, :] = k1.astype(BF16)
    gat[0, 0, p, 192:320, :] = total_v.astype(BF16)

    pl.semaphore_wait(barrier, 2 * CN - 1)

    def to_z(dz):
        return remote(
            gat.at[0, 0, p],
            gat.at[0, ZN - dz, p],
            z_send.at[dz],
            g_recv.at[0, ZN - dz, p],
            at(0, dz),
            p,
        )

    def to_x(zr, up):
        return remote(
            gat.at[0, zr, p],
            gat.at[3 if up else 1, zr, p],
            x_send.at[zr, 0 if up else 1],
            g_recv.at[3 if up else 1, zr, p],
            at(1 if up else -1, 0),
            p,
        )

    def to_x2(zr):
        near_row = 3 - 2 * p
        return remote(
            gat.at[near_row, zr, p],
            gat.at[2, zr, p],
            x2_send.at[zr],
            g_recv.at[2, zr, p],
            at(1 - 2 * p, 0),
            p,
        )

    def to_d(xr, zr):
        return remote(
            gat.at[xr, zr, p],
            gat.at[xr, zr, p],
            d_send.at[xr, zr],
            g_recv.at[xr, zr, p],
            ctx,
            other,
        )

    def arrive(xr, zr, q):
        remote(
            gat.at[xr, zr, q], gat.at[xr, zr, q], d_send.at[xr, zr], g_recv.at[xr, zr, q], ctx, other
        ).wait_recv()

    for dz in (1, 7, 2, 6, 3, 5, 4):
        to_z(dz).start()
    to_x(0, True).start()
    to_x(0, False).start()
    to_d(0, 0).start()

    def to_w(k):
        f = flat + k
        return remote(
            win.at[4], win.at[4 - k], w_send.at[k - 1], w_recv.at[k - 1], f // 2, lax.rem(f, 2)
        )

    for k in range(1, 5):

        @pl.when(flat + k < 2 * CN)
        def _():
            to_w(k).start()

    def store_block(ref, at_index, number):
        a0, a1 = pack_keys(ck[number].astype(F32))
        ref[at_index, 0:64, :] = a0.astype(BF16)
        ref[at_index, 64:96, :] = a1.astype(BF16)
        ref[at_index, 96:160, :] = cv[number]

    def first_fixed(i):
        return remote(
            recv.at[64],
            recv.at[64],
            f_send.at[i],
            f_recv.at[0],
            lax.rem(ctx + i, CN),
            p,
        )

    def last_fixed(i):
        return remote(
            recv.at[pl.ds(65, 2)],
            recv.at[pl.ds(65, 2)],
            f_send.at[i],
            f_recv.at[1],
            lax.rem(ctx + i, CN),
            p,
        )

    def start_all(make):
        def one(i, carry):
            make(i).start()
            return carry

        lax.fori_loop(1, CN, one, 0)

    def sent_all(make):
        def one(i, carry):
            make(i).wait_send()
            return carry

        lax.fori_loop(1, CN, one, 0)

    @pl.when(ctx == 0)
    def _():
        store_block(recv, 64, 0)
        start_all(first_fixed)

    @pl.when(ctx == CN - 1)
    def _():
        store_block(recv, 65, SBLK - 2)
        store_block(recv, 66, SBLK - 1)
        start_all(last_fixed)

    def to_a(i):
        dx, dz = i // ZN, lax.rem(i, ZN)
        back = lax.rem(XN - dx, XN) * ZN + lax.rem(ZN - dz, ZN)
        return remote(
            send.at[pl.ds(2 * i, 2)],
            recv.at[pl.ds(2 * back, 2)],
            a_send.at[i],
            a_recv.at[back],
            at(dx, dz),
            p,
        )

    for j in range(2):
        store_block(recv, j, asked[ctx, j])

    def fill(i, carry):
        c = at(i // ZN, lax.rem(i, ZN))
        for j in range(2):
            store_block(send, 2 * i + j, asked[c, j])
        to_a(i).start()
        return carry

    lax.fori_loop(1, CN, fill, 0)

    lane = lax.broadcasted_iota(jnp.int32, (UNIT, 256), 1)
    gates = [jax.nn.sigmoid(gl[i]) for i in range(3)]
    for pair in range(HEADS // 2):
        both = queries[:, pair * 384 : (pair + 1) * 384].astype(F32)
        first = jnp.where(lane < DK, both[:, 0:256], 0.0).astype(BF16)
        second = jnp.where(lane < DK, pltpu.roll(both[:, 128:384], 192, 1), 0.0).astype(BF16)
        for h, rows in ((2 * pair, first), (2 * pair + 1, second)):
            for b in range(2):
                base = b * 1024 + h * 64
                qs[base : base + 64, :] = rows[b * 64 : b * 64 + 64]
                for i in range(3):
                    gate[i, base : base + 64, :] = jnp.broadcast_to(
                        gates[i][b * 64 : b * 64 + 64, h : h + 1], (64, 128)
                    )
    vt[:, 128:256] = jnp.ones((1024, 128), BF16)

    def unpack(ref_at, n, base):
        half = ref_at[n : n + n // 2, :]
        kt[base : base + n, 0:128] = ref_at[0:n, :]
        kt[base : base + n // 2, 128:256] = half
        kt[base + n // 2 : base + n, 128:256] = pltpu.roll(half.astype(F32), 64, 1).astype(BF16)
        vt[base : base + n, 0:128] = ref_at[n + n // 2 : 2 * n + n // 2, :]

    for k in range(1, 5):

        @pl.when(flat >= k)
        def _():
            remote(
                win.at[4 - k], win.at[4 - k], w_send.at[k - 1], w_recv.at[k - 1], ctx, other
            ).wait_recv()

    for k in range(5):
        unpack(win.at[k], UNIT, k * UNIT)

    def window_chunk(r, carry):
        rows = pl.ds(pl.multiple_of(r * CHUNK, CHUNK), CHUNK)
        width = WINDOW + UNIT
        s = dot_t(qs[rows, :], kt[0:width, :])
        i_at = lax.rem(lax.broadcasted_iota(jnp.int32, (CHUNK, width), 0), 64)
        j_at = lax.broadcasted_iota(jnp.int32, (CHUNK, width), 1)
        dist = WINDOW + (r // 2) * 64 + i_at - j_at
        allowed = (dist >= 0) & (dist < WINDOW) & (j_at >= WINDOW - flat * UNIT)
        s = jnp.where(allowed, s * CEXP, LOW)
        e = jnp.exp2(s - jnp.max(s, axis=1, keepdims=True)).astype(BF16)
        o = jnp.dot(e, vt[0:width, :], preferred_element_type=F32)
        mixed[rows, :] = gate[2, rows, :] * (o[:, 0:128] / o[:, 128:256])
        peak[rows, :] = jnp.full((CHUNK, 128), LOW, F32)
        acc[rows, :] = jnp.zeros((CHUNK, 256), F32)
        return carry

    lax.fori_loop(0, ROWS // CHUNK, window_chunk, 0)

    def tile(xr, zs):
        for n, zr in enumerate(zs):
            for q in range(2):
                unpack(gat.at[xr, zr, q], UNIT, n * 256 + q * UNIT)

        def chunk(r, carry):
            rows = pl.ds(pl.multiple_of(r * CHUNK, CHUNK), CHUNK)
            s = dot_t(qs[rows, :], kt[...])
            before = peak[rows, :]
            top = jnp.maximum(before, jnp.max(s, axis=1, keepdims=True) * CEXP)
            e = jnp.exp2(s * CEXP - top[:, 0:1]).astype(BF16)
            factor = jnp.exp2(before - top)
            o = jnp.dot(e, vt[...], preferred_element_type=F32)
            acc[rows, 0:128] = acc[rows, 0:128] * factor + o[:, 0:128]
            acc[rows, 128:256] = acc[rows, 128:256] * factor + o[:, 128:256]
            peak[rows, :] = top
            return carry

        lax.fori_loop(0, ROWS // CHUNK, chunk, 0)

    for zs in (NEAR, FAR):
        for zr in zs:
            if zr:
                arrive(0, zr, p)
                to_x(zr, True).start()
                to_x(zr, False).start()
                to_d(0, zr).start()
        for zr in zs:
            arrive(0, zr, other)
        tile(0, zs)
    for zs in (NEAR, FAR):
        for zr in zs:
            arrive(3, zr, p)
            to_d(3, zr).start()
            arrive(1, zr, p)
            to_d(1, zr).start()
            to_x2(zr).start()
        for xr in (3, 1):
            for zr in zs:
                arrive(xr, zr, other)
            tile(xr, zs)
    for zs in (NEAR, FAR):
        for zr in zs:
            arrive(2, zr, p)
            to_d(2, zr).start()
        for zr in zs:
            arrive(2, zr, other)
        tile(2, zs)

    def settle(r, carry):
        rows = pl.ds(pl.multiple_of(r * CHUNK, CHUNK), CHUNK)
        mixed[rows, :] += gate[0, rows, :] * (acc[rows, 0:128] / acc[rows, 128:256])
        return carry

    lax.fori_loop(0, ROWS // CHUNK, settle, 0)

    def got_a(i, carry):
        remote(
            send.at[pl.ds(2 * i, 2)], recv.at[pl.ds(2 * i, 2)], a_send.at[i], a_recv.at[i], ctx, other
        ).wait_recv()
        return carry

    lax.fori_loop(1, CN, got_a, 0)

    @pl.when(ctx != 0)
    def _():
        first_fixed(1).wait_recv()

    @pl.when(ctx != CN - 1)
    def _():
        last_fixed(1).wait_recv()

    for b in range(2):
        for n in range(16):
            number = 64 + n if n < 3 else picks[b, n - 3]
            block = recv[number]
            kt[n * 64 : n * 64 + 64, 0:128] = block[0:64]
            kt[n * 64 : n * 64 + 32, 128:256] = block[64:96]
            kt[n * 64 + 32 : n * 64 + 64, 128:256] = pltpu.roll(
                block[64:96].astype(F32), 64, 1
            ).astype(BF16)
            vt[n * 64 : n * 64 + 64, 0:128] = block[96:160]
        for r in range(1024 // CHUNK):
            base = b * 1024 + r * CHUNK
            rows = pl.ds(base, CHUNK)
            s = dot_t(qs[rows, :], kt[...]) * CEXP
            e = jnp.exp2(s - jnp.max(s, axis=1, keepdims=True)).astype(BF16)
            o = jnp.dot(e, vt[...], preferred_element_type=F32)
            done = mixed[rows, :] + gate[1, rows, :] * (o[:, 0:128] / o[:, 128:256])
            for h in range(CHUNK // 64):
                head = r * (CHUNK // 64) + h
                out[b * 64 : b * 64 + 64, head * 128 : head * 128 + 128] = done[
                    h * 64 : h * 64 + 64
                ].astype(BF16)

    for dz in range(1, ZN):
        to_z(dz).wait_send()
    for zr in range(ZN):
        to_x(zr, True).wait_send()
        to_x(zr, False).wait_send()
        to_x2(zr).wait_send()
        for xr in range(XN):
            to_d(xr, zr).wait_send()
    for k in range(1, 5):

        @pl.when(flat + k < 2 * CN)
        def _():
            to_w(k).wait_send()

    sent_all(to_a)

    @pl.when(ctx == 0)
    def _():
        sent_all(first_fixed)

    @pl.when(ctx == CN - 1)
    def _():
        sent_all(last_fixed)


def wanted(listed):
    ids = listed.reshape(-1)
    owner = ids // SBLK
    place = jnp.arange(ids.shape[0], dtype=jnp.int32)
    before = (owner[None, :] == owner[:, None]) & (place[None, :] < place[:, None])
    rank = jnp.sum(before.astype(jnp.int32), axis=1)
    slots = owner * 2 + rank
    cells = jnp.arange(CN * 2, dtype=jnp.int32)
    table = jnp.sum(jnp.where(slots[:, None] == cells[None, :], (ids % SBLK)[:, None], 0), axis=0)
    return owner, rank, table.reshape(CN, 2)


def on_device(queries, sk, sv, pk, cv, lengths, cw, selections, gl):
    listed = selections[:, 0, :]
    owner, rank, table = wanted(listed)
    asked = lax.all_to_all(table, "ctx", split_axis=0, concat_axis=0, tiled=True)
    ctx = lax.axis_index("ctx")
    rel = ((owner // ZN - ctx // ZN) % XN) * ZN + (owner % ZN - ctx % ZN) % ZN
    picks = (rel * 2 + rank).reshape(listed.shape)
    blocks = pk.shape[0] // SBLK
    vmem = pl.BlockSpec(memory_space=pltpu.VMEM)
    smem = pl.BlockSpec(memory_space=pltpu.SMEM)
    dma = pltpu.SemaphoreType.DMA
    return pl.pallas_call(
        body,
        name="attend",
        out_shape=jax.ShapeDtypeStruct((queries.shape[0], HEADS * DV), BF16),
        in_specs=[smem] * 3 + [vmem] * 7,
        out_specs=vmem,
        scratch_shapes=[
            pltpu.VMEM((XN, ZN, 2, PACK, 128), BF16),
            pltpu.VMEM((2 * CN, SPACK, 128), BF16),
            pltpu.VMEM((2 * CN + 3, SPACK, 128), BF16),
            pltpu.VMEM((5, PACK, 128), BF16),
            pltpu.VMEM((ROWS, 256), BF16),
            pltpu.VMEM((ROWS, 256), F32),
            pltpu.VMEM((ROWS, 128), F32),
            pltpu.VMEM((ROWS, 128), F32),
            pltpu.VMEM((3, ROWS, 128), F32),
            pltpu.VMEM((1024, 256), BF16),
            pltpu.VMEM((1024, 256), BF16),
            dma((ZN,)),
            dma((ZN, 2)),
            dma((ZN,)),
            dma((XN, ZN)),
            dma((XN, ZN, 2)),
            dma((CN,)),
            dma((CN,)),
            dma((4,)),
            dma((4,)),
            dma((CN,)),
            dma((2,)),
        ],
        compiler_params=pltpu.CompilerParams(
            collective_id=0, has_side_effects=True, vmem_limit_bytes=60 * 1024 * 1024
        ),
    )(
        asked,
        picks,
        cw,
        lengths,
        queries,
        sk,
        sv,
        pk.reshape(blocks, SBLK, DK),
        cv.reshape(blocks, SBLK, DV),
        gl,
    )


def solution(mesh):
    placed = (
        P(("ctx", "pb"), "ga"),
        P(("ctx", "pb"), "ga"),
        P(("ctx", "pb"), "ga"),
        P("ctx", "ga"),
        P("ctx", "ga"),
        P("ctx", None),
        P("ga", None),
        P(("ctx", "pb"), "ga", None),
        P(None, ("ctx", "pb"), "ga"),
    )
    return jax.shard_map(
        on_device, mesh=mesh, in_specs=placed, out_specs=P(("ctx", "pb"), "ga"), check_vma=False
    )
```

time: 365 us -> 152 us (0.42)
  the two profiles are of different devices: /device:TPU:1 before, /device:TPU:89 now
where the time goes in v1:
time: 152 us
  Pallas kernels  128 us (84%)
  local copies, waits for them, and re-layouts  10.8 us (7%)
  starting transfers between devices  10.2 us (7%)
  other arithmetic  2.93 us (2%)
    pallas_call x1, Pallas kernels, on_device(): pl.pallas_call(body, name='attend', out_shape=jax.ShapeDtypeStruct((queri...  128 us
    all_to_all x1, starting transfers between devices, on_device(): lax.all_to_all(table, 'ctx', split_axis=0, concat_axis=0, tiled=True)  10.2 us
    unnamed x7, local copies, waits for them, and re-layouts  9.92 us
  transfers between devices with their start and end apart: 1, of which 0 were waited for; matrix products, arithmetic and copies ran while one was open for 5% of the time, Pallas kernels for 0%

profile of v1, /device:TPU:89, one launch (start us, length us, event | category | flops | bytes accessed | tf_op | source)
XLA Modules:
  0.0 151.9 jit_solution(15741793580528441117)
XLA Ops:
  0.0 0.5 broadcast.185
  0.5 1.3 reduce.3
  1.9 0.1 reshape_squeeze.5
  2.0 0.2 convert_reduce_fusion
  2.1 0.1 select_reduce_fusion
  2.2 0.7 all_to_all.7
  2.9 10.2 %all-to-all-start = ((s32[32,1,2]{2,1,0:T(1,128)}), s32[32,1,2]{2,1,0:T(1,128)S(1)}, u32[]{:S(2)}, u32[]{:S(2)}) async-start(s32[32,1,2]{2,1,0:T(1,128)} %bitcast), calls=%async_computation | async-start | bytes 32768 | tf_op jit(solution)/shard_map/all_to_all | solution.py:472
  13.1 0.1 reduce_sum.22
  13.2 1.3 multiply_add_fusion.picks
  14.5 1.5 copy.30.sk
  16.0 1.5 %copy.31.gl = f32[3,128,16]{2,1,0:T(8,128)} copy(f32[3,128,16]{1,2,0:T(8,128)} %param.17) | data formatting | bytes 49152 | tf_op args[8]
  17.6 3.9 %copy.28 = bf16[4096,192]{1,0:T(8,128)(2,1)} copy(bf16[4096,192]{0,1:T(8,128)(2,1)} %param.12) | data formatting | bytes 3145728 | tf_op args[3]
  21.4 0.0 all-to-all-done
  21.5 0.0 copy-start
  21.5 0.6 copy-done
  22.1 127.9 %attend.1 = bf16[128,2048]{1,0:T(8,128)(2,1)} custom-call(s32[32,2]{1,0:T(8,128)} %bitcast.7, s32[2,13]{1,0:T(2,128)} %multiply_add_fusion.picks, f32[1,32]{1,0:T(1,128)} %cw.1, s32[1,256]{1,0:T(1,128)} %lengths.1, bf16[128,3072]{1,0:T(8,128)(2,1)} %queries.1, bf16[128,192]{1,0:T(8,128)(2,1)} %copy.30.sk, bf16[128,128]{1,0:T(8,128)(2,1)} %sv.1, ...), custom_call_target="tpu_custom_call" | custom-call | tf_op jit(solution)/shard_map/attend/pallas_call | solution.py:480
  150.0 1.9 %copy.34 = bf16[128,2048]{1,0:T(8,128)(2,1)} copy(bf16[128,2048]{1,0:T(8,128)(2,1)} %attend.1) | data formatting | bytes 1048576
  (2 shorter events, 0.0 us)
Async XLA Ops:
  2.9 18.5 %all-to-all-start = ((s32[32,1,2]{2,1,0:T(1,128)}), s32[32,1,2]{2,1,0:T(1,128)S(1)}, u32[]{:S(2)}, u32[]{:S(2)}) async-start(s32[32,1,2]{2,1,0:T(1,128)} %bitcast), calls=%async_computation | async-start | bytes 32768 | tf_op jit(solution)/shard_map/all_to_all | solution.py:472
  21.5 0.6 copy-start

commit v2 on v1

v2 whole, which is shorter than its diff:
```python
import functools
import math

import jax
import jax.numpy as jnp
from jax import lax
from jax.experimental import pallas as pl
from jax.experimental.pallas import tpu as pltpu
from jax.sharding import PartitionSpec as P

SBLK = 64
WINDOW = 512
XN, ZN = 4, 8
CN = XN * ZN
HEADS = 16
DK, DV = 192, 128
UNIT = 128
PACK = UNIT * 5 // 2
SPACK = SBLK * 5 // 2
ZSET = ((0, 1, 7, 2), (6, 3, 5, 4))
ORDER = ((0, 0), (0, 1), (3, 0), (1, 0), (3, 1), (1, 1), (2, 0), (2, 1))
PACE = (3, 3, 4, 4, 4, 4, 4, 5)
ROWS = 2048
CHUNK = 512
MESH = pl.DeviceIdType.MESH
LOW = -1e30
CEXP = math.log2(math.e) / math.sqrt(DK)
F32 = jnp.float32
BF16 = jnp.bfloat16


def pack_keys(k):
    n = k.shape[0]
    tail = k[:, 128:192]
    return k[:, :128], jnp.concatenate([tail[: n // 2], tail[n // 2 :]], axis=1)


def dot_t(a, b):
    return lax.dot_general(a, b, (((1,), (1,)), ((), ())), preferred_element_type=F32)


def slot(xr, zr):
    far = 0 if zr in ZSET[0] else 1
    return ORDER.index((xr, far)), ZSET[far].index(zr)


def body(
    cw,
    sel_s,
    sel,
    lengths,
    queries,
    sk,
    sv,
    ck,
    cv,
    gl,
    out,
    gat,
    send,
    recv,
    win,
    mine,
    reqs,
    offs,
    asked,
    qs,
    acc,
    peak,
    mixed,
    gate,
    kt,
    vt,
    vr,
    sbuf,
    z_send,
    x_send,
    x2_send,
    d_send,
    g_recv,
    a_send,
    a_recv,
    w_send,
    wd_send,
    w_recv,
    f_send,
    f_recv,
    q_send,
    q_recv,
    l_sem,
):
    ctx = lax.axis_index("ctx")
    p = lax.axis_index("pb")
    x = ctx // ZN
    z = lax.rem(ctx, ZN)
    flat = ctx * 2 + p
    other = 1 - p

    def at(dx, dz):
        return lax.rem(x + dx + XN, XN) * ZN + lax.rem(z + dz + ZN, ZN)

    def remote(src, dst, ssem, rsem, c, q):
        return pltpu.make_async_remote_copy(
            src_ref=src,
            dst_ref=dst,
            send_sem=ssem,
            recv_sem=rsem,
            device_id={"ctx": c, "pb": q},
            device_id_type=MESH,
        )

    barrier = pltpu.get_barrier_semaphore()

    def greet(i, carry):
        c = lax.rem(ctx + i // 2, CN)
        q = lax.rem(p + lax.rem(i, 2), 2)
        pl.semaphore_signal(barrier, inc=1, device_id={"ctx": c, "pb": q}, device_id_type=MESH)
        return carry

    lax.fori_loop(1, 2 * CN, greet, 0)

    mine[...] = jnp.full((2, 1, 128), -1, jnp.int32)
    for b in range(2):
        mine[b, :, 0:13] = sel[b]
    reqs[0] = jnp.full((2, 1, 128), -1, jnp.int32)
    for b in range(2):
        reqs[0, b, :, 0:13] = sel[b]
    k0, k1 = pack_keys(sk[...].astype(F32))
    win[0, p, 0:128, :] = k0.astype(BF16)
    win[0, p, 128:192, :] = k1.astype(BF16)
    win[0, p, 192:320, :] = sv[...].astype(F32).T.astype(BF16)
    for k in range(1, 3):

        @pl.when(ctx < k)
        def _():
            win[k] = jnp.zeros((2, PACK, 128), BF16)

    b_at = p * UNIT + lax.broadcasted_iota(jnp.int32, (UNIT, 256), 0)
    j_at = lax.broadcasted_iota(jnp.int32, (UNIT, 256), 1)
    n_row = jnp.broadcast_to(lengths[...], (UNIT, 256)).astype(F32)
    starts = jnp.sum(jnp.where(j_at < b_at, n_row, 0.0), axis=1, keepdims=True)
    counts = jnp.sum(jnp.where(j_at == b_at, n_row, 0.0), axis=1, keepdims=True)
    spread = 1.0 / jnp.sqrt(counts)
    span = ck.shape[0] * SBLK
    step = 512
    total_k = jnp.zeros((UNIT, DK), F32)
    total_v = jnp.zeros((UNIT, DV), F32)
    for t in range(0, span, step):
        pos = (lax.broadcasted_iota(jnp.int32, (UNIT, step), 1) + t).astype(F32)
        away = pos - starts
        member = (away >= 0.0) & (away < counts)
        off = jnp.sum(jnp.where(member, away, 0.0), axis=0, keepdims=True)
        weight = jnp.zeros((1, step), F32)
        for i in range(32):
            weight = jnp.where(off == float(i), cw[0, i], weight)
        matrix = jnp.where(member, weight * spread, 0.0).astype(BF16)
        rows = ck[t // SBLK : (t + step) // SBLK].reshape(step, DK)
        vals = cv[t // SBLK : (t + step) // SBLK].reshape(step, DV)
        total_k += jnp.dot(matrix, rows, preferred_element_type=F32)
        total_v += jnp.dot(matrix, vals, preferred_element_type=F32)
    k0, k1 = pack_keys(total_k)
    gat[0, 0, p, 0:128, :] = k0.astype(BF16)
    gat[0, 0, p, 128:192, :] = k1.astype(BF16)
    gat[0, 0, p, 192:320, :] = total_v.T.astype(BF16)

    pl.semaphore_wait(barrier, 2 * CN - 1)

    def to_q(i):
        dx, dz = i // ZN, lax.rem(i, ZN)
        back = lax.rem(XN - dx, XN) * ZN + lax.rem(ZN - dz, ZN)
        return remote(mine, reqs.at[back], q_send.at[i], q_recv.at[back], at(dx, dz), p)

    def got_q(i, carry):
        remote(mine, reqs.at[i], q_send.at[i], q_recv.at[i], ctx, other).wait_recv()
        return carry

    def start_all(make):
        def one(i, carry):
            make(i).start()
            return carry

        lax.fori_loop(1, CN, one, 0)

    def sent_all(make):
        def one(i, carry):
            make(i).wait_send()
            return carry

        lax.fori_loop(1, CN, one, 0)

    start_all(to_q)

    def g_at(xr, zr, q):
        t, n = slot(xr, zr)
        return gat.at[t, n, q]

    def g_sem(xr, zr, q):
        t, n = slot(xr, zr)
        return g_recv.at[t, n, q]

    def to_z(zr, up):
        return remote(
            g_at(0, zr, p),
            g_at(0, (zr + (7 if up else 1)) % ZN, p),
            z_send.at[zr, 0 if up else 1],
            g_sem(0, (zr + (7 if up else 1)) % ZN, p),
            at(0, 1 if up else -1),
            p,
        )

    def to_x(zr, up):
        return remote(
            g_at(0, zr, p),
            g_at(3 if up else 1, zr, p),
            x_send.at[zr, 0 if up else 1],
            g_sem(3 if up else 1, zr, p),
            at(1 if up else -1, 0),
            p,
        )

    def to_x2(zr):
        t3, n = slot(3, zr)
        t1, _ = slot(1, zr)
        return remote(
            gat.at[t3 + p * (t1 - t3), n, p],
            g_at(2, zr, p),
            x2_send.at[zr],
            g_sem(2, zr, p),
            at(1 - 2 * p, 0),
            p,
        )

    def to_d(xr, zr):
        return remote(
            g_at(xr, zr, p), g_at(xr, zr, p), d_send.at[xr, zr], g_sem(xr, zr, p), ctx, other
        )

    def arrive(xr, zr, q):
        remote(
            g_at(xr, zr, q), g_at(xr, zr, q), d_send.at[xr, zr], g_sem(xr, zr, q), ctx, other
        ).wait_recv()

    def spread_on(zr):
        if zr in (0, 7, 6):
            to_z(zr, True).start()
        if zr in (0, 1, 2):
            to_z(zr, False).start()
        if zr == 5:

            @pl.when(p == 0)
            def _():
                to_z(5, True).start()

        if zr == 3:

            @pl.when(p == 1)
            def _():
                to_z(3, False).start()

        to_x(zr, True).start()
        to_x(zr, False).start()
        to_d(0, zr).start()

    spread_on(0)

    def to_w(k):
        return remote(
            win.at[k, p], win.at[k + 1, p], w_send.at[k], w_recv.at[k + 1, p], lax.rem(ctx + 1, CN), p
        )

    def to_wd(k):
        return remote(win.at[k, p], win.at[k, p], wd_send.at[k], w_recv.at[k, p], ctx, other)

    def got_w(k, q):
        remote(win.at[k, q], win.at[k, q], wd_send.at[k], w_recv.at[k, q], ctx, other).wait_recv()

    @pl.when(ctx + 1 < CN)
    def _():
        to_w(0).start()

    to_wd(0).start()

    def store_block(ref, at_index, number):
        a0, a1 = pack_keys(ck[number].astype(F32))
        ref[at_index, 0:64, :] = a0.astype(BF16)
        ref[at_index, 64:96, :] = a1.astype(BF16)
        ref[at_index, 96:160, :] = cv[number]

    def first_fixed(i):
        return remote(
            recv.at[64], recv.at[64], f_send.at[i], f_recv.at[0], lax.rem(ctx + i, CN), p
        )

    def last_fixed(i):
        return remote(
            recv.at[pl.ds(65, 2)],
            recv.at[pl.ds(65, 2)],
            f_send.at[i],
            f_recv.at[1],
            lax.rem(ctx + i, CN),
            p,
        )

    @pl.when(ctx == 0)
    def _():
        store_block(recv, 64, 0)
        start_all(first_fixed)

    @pl.when(ctx == CN - 1)
    def _():
        store_block(recv, 65, SBLK - 2)
        store_block(recv, 66, SBLK - 1)
        start_all(last_fixed)

    lane = lax.broadcasted_iota(jnp.int32, (UNIT, 256), 1)
    for pair in range(HEADS // 2):
        both = queries[:, pair * 384 : (pair + 1) * 384].astype(F32)
        first = jnp.where(lane < DK, both[:, 0:256], 0.0).astype(BF16)
        second = jnp.where(lane < DK, pltpu.roll(both[:, 128:384], 192, 1), 0.0).astype(BF16)
        for h, rows in ((2 * pair, first), (2 * pair + 1, second)):
            for b in range(2):
                base = b * 1024 + h * 64
                qs[base : base + 64, :] = rows[b * 64 : b * 64 + 64]

    lfn = pltpu.make_async_copy(offs, asked, l_sem)
    lax.fori_loop(1, CN, got_q, 0)
    big = 1 << 20
    lanes = lax.broadcasted_iota(jnp.int32, (CN, 1, 128), 2)
    keys = []
    for b in range(2):
        ids = reqs[:, b]
        here = (ids >= ctx * SBLK) & (ids < (ctx + 1) * SBLK)
        keys.append(jnp.where(here, b * 8192 + lanes * SBLK + ids - ctx * SBLK, big))
    one = jnp.min(jnp.minimum(keys[0], keys[1]), axis=2, keepdims=True)
    rest = [jnp.where(k > one, k, big) for k in keys]
    two = jnp.min(jnp.minimum(rest[0], rest[1]), axis=2, keepdims=True)
    offs[...] = jnp.where(lanes == 0, one, two) & (SBLK - 1)
    lfn.start()

    lane = lax.broadcasted_iota(jnp.int32, (8, 128), 1)
    for i in range(3):
        g = jax.nn.sigmoid(gl[i])
        turned = pltpu.roll(g, 64, 1)
        for b in range(2):
            for h in range(0, HEADS, 2):
                low = (g, turned)[b][h : h + 1]
                high = (turned, g)[b][h + 1 : h + 2]
                c, n = b * 2 + h // 8, (h % 8) * 64
                gate[i, c, :, n : n + 128] = jnp.where(lane < 64, low, high)
    vt[128:144, :] = jnp.ones((16, 1024), BF16)

    def unpack_keys(ref_at, n, base):
        half = ref_at[n : n + n // 2, :]
        kt[base : base + n, 0:128] = ref_at[0:n, :]
        kt[base : base + n // 2, 128:256] = half
        kt[base + n // 2 : base + n, 128:256] = pltpu.roll(half.astype(F32), 64, 1).astype(BF16)

    def unpack(ref_at, base):
        unpack_keys(ref_at, UNIT, base)
        vt[0:128, base : base + UNIT] = ref_at[192:320, :]

    lfn.wait()

    def to_a(i):
        dx, dz = i // ZN, lax.rem(i, ZN)
        back = lax.rem(XN - dx, XN) * ZN + lax.rem(ZN - dz, ZN)
        return remote(
            send.at[pl.ds(2 * i, 2)],
            recv.at[pl.ds(2 * back, 2)],
            a_send.at[i],
            a_recv.at[back],
            at(dx, dz),
            p,
        )

    for j in range(2):
        store_block(recv, j, asked[0, 0, j])

    def fill(n, carry):
        i = lax.rem(n * 5, CN)
        for j in range(2):
            store_block(send, 2 * i + j, asked[i, 0, j])
        to_a(i).start()
        return carry

    def listed(stage):
        lax.fori_loop(1 + sum(PACE[:stage]), 1 + sum(PACE[: stage + 1]), fill, 0)

    listed(0)

    for zr in (1, 7):
        arrive(0, zr, p)
        spread_on(zr)

    @pl.when(ctx >= 1)
    def _():
        got_w(1, p)
        to_wd(1).start()

        @pl.when(ctx + 1 < CN)
        def _():
            to_w(1).start()

    listed(1)

    for zr in (2, 6):
        arrive(0, zr, p)
        spread_on(zr)

    @pl.when(ctx >= 2)
    def _():
        got_w(2, p)
        to_wd(2).start()

    got_w(0, other)
    for k in (1, 2):

        @pl.when(ctx >= k)
        def _():
            got_w(k, other)

    for k in range(5):
        unpack(win.at[2 - (p + k) // 2, lax.rem(p + k, 2)], k * UNIT)
    near = WINDOW + UNIT

    def scores(c, width):
        return dot_t(kt[0:width, :], qs[c * CHUNK : (c + 1) * CHUNK, :])

    def mix(e, width):
        return jnp.dot(vt[:, 0:width], e, preferred_element_type=F32)

    sbuf[0, 0:near, :] = scores(0, near)
    for c in range(4):
        if c < 3:
            sbuf[(c + 1) % 2, 0:near, :] = scores(c + 1, near)
        i_at = lax.broadcasted_iota(jnp.int32, (near, CHUNK), 1) & 63
        j_at = lax.broadcasted_iota(jnp.int32, (near, CHUNK), 0)
        dist = WINDOW + (c // 2) * 64 + i_at - j_at
        allowed = (dist >= 0) & (dist < WINDOW) & (j_at >= WINDOW - flat * UNIT)
        sc = jnp.where(allowed, sbuf[c % 2, 0:near, :] * CEXP, LOW)
        e = jnp.exp2(sc - jnp.max(sc, axis=0, keepdims=True)).astype(BF16)
        o = mix(e, near)
        mixed[c] = o[0:128] * (gate[2, c, 0:1] / o[128:129])
        peak[c] = jnp.full((8, CHUNK), LOW, F32)
        acc[c] = jnp.zeros((144, CHUNK), F32)

    def stage(t):
        if t == 0:
            for zr in (3, 5):
                arrive(0, zr, p)
                spread_on(zr)
            need = [(0, zr) for zr in ZSET[0]]
        elif t == 1:
            arrive(0, 4, p)
            spread_on(4)
            need = [(0, zr) for zr in ZSET[1]]
        else:
            xr, far = ORDER[t]
            need = [(xr, zr) for zr in ZSET[far]]
            if xr == 3:
                for zr in ZSET[far]:
                    arrive(3, zr, p)
                    to_d(3, zr).start()
                    arrive(1, zr, p)
                    to_d(1, zr).start()
                    to_x2(zr).start()
            elif xr == 2:
                for zr in ZSET[far]:
                    arrive(2, zr, p)
                    to_d(2, zr).start()
        if t < 6:
            listed(t + 2)
        for xr, zr in need:
            arrive(xr, zr, other)

    def tile(t, carry):
        for k in range(8):

            @pl.when(t == k)
            def _():
                stage(k)

        for n in range(4):
            for q in range(2):
                unpack(gat.at[t, n, q], n * 256 + q * UNIT)
        sbuf[0] = scores(0, 1024)
        for c in range(4):
            if c < 3:
                sbuf[(c + 1) % 2] = scores(c + 1, 1024)
            sc = sbuf[c % 2]
            before = peak[c]
            top = jnp.maximum(before, jnp.max(sc, axis=0, keepdims=True) * CEXP)
            e = jnp.exp2(sc * CEXP - top[0:1]).astype(BF16)
            factor = jnp.exp2(before - top)[0:1]
            acc[c] = acc[c] * factor + mix(e, 1024)
            peak[c] = top
        return carry

    lax.fori_loop(0, 8, tile, 0)

    for c in range(4):
        mixed[c] += acc[c, 0:128] * (gate[0, c, 0:1] / acc[c, 128:129])

    def got_a(i, carry):
        remote(
            send.at[pl.ds(2 * i, 2)], recv.at[pl.ds(2 * i, 2)], a_send.at[i], a_recv.at[i], ctx, other
        ).wait_recv()
        return carry

    lax.fori_loop(1, CN, got_a, 0)

    @pl.when(ctx != 0)
    def _():
        first_fixed(1).wait_recv()

    @pl.when(ctx != CN - 1)
    def _():
        last_fixed(1).wait_recv()

    ids = [sel_s[b, 0, n] for b in range(2) for n in range(13)]
    owner = [i // SBLK for i in ids]
    picks = []
    for n, own in enumerate(owner):
        rank = 0
        for m in range(n):
            rank = rank + jnp.where(owner[m] == own, 1, 0)
        ox, oz = own // ZN, own % ZN
        rel = ((ox + XN - x) % XN) * ZN + (oz + ZN - z) % ZN
        picks.append(rel * 2 + jnp.minimum(rank, 1))
    for b in range(2):
        for n in range(16):
            number = 64 + n if n < 3 else picks[b * 13 + n - 3]
            block = recv[number]
            unpack_keys(block, SBLK, n * SBLK)
            vr[n * 64 : n * 64 + 64, :] = block[96:160]
        vt[0:128, :] = vr[...].T
        sbuf[0] = scores(2 * b, 1024)
        for r in range(2):
            if r == 0:
                sbuf[1] = scores(2 * b + 1, 1024)
            c = 2 * b + r
            sc = sbuf[r] * CEXP
            e = jnp.exp2(sc - jnp.max(sc, axis=0, keepdims=True)).astype(BF16)
            o = mix(e, 1024)
            done = (mixed[c] + o[0:128] * (gate[1, c, 0:1] / o[128:129])).T
            for h in range(CHUNK // 64):
                head = r * (CHUNK // 64) + h
                out[b * 64 : b * 64 + 64, head * 128 : head * 128 + 128] = done[
                    h * 64 : h * 64 + 64
                ].astype(BF16)

    for zr in (0, 7, 6):
        to_z(zr, True).wait_send()
    for zr in (0, 1, 2):
        to_z(zr, False).wait_send()

    @pl.when(p == 0)
    def _():
        to_z(5, True).wait_send()

    @pl.when(p == 1)
    def _():
        to_z(3, False).wait_send()

    for zr in range(ZN):
        to_x(zr, True).wait_send()
        to_x(zr, False).wait_send()
        to_x2(zr).wait_send()
        for xr in range(XN):
            to_d(xr, zr).wait_send()
    to_wd(0).wait_send()

    @pl.when(ctx + 1 < CN)
    def _():
        to_w(0).wait_send()

    @pl.when(ctx >= 1)
    def _():
        to_wd(1).wait_send()

        @pl.when(ctx + 1 < CN)
        def _():
            to_w(1).wait_send()

    @pl.when(ctx >= 2)
    def _():
        to_wd(2).wait_send()

    sent_all(to_q)
    sent_all(to_a)

    @pl.when(ctx == 0)
    def _():
        sent_all(first_fixed)

    @pl.when(ctx == CN - 1)
    def _():
        sent_all(last_fixed)


def on_device(queries, sk, sv, pk, cv, lengths, cw, selections, gl):
    blocks = pk.shape[0] // SBLK
    vmem = pl.BlockSpec(memory_space=pltpu.VMEM)
    smem = pl.BlockSpec(memory_space=pltpu.SMEM)
    dma = pltpu.SemaphoreType.DMA
    return pl.pallas_call(
        body,
        name="attend",
        out_shape=jax.ShapeDtypeStruct((queries.shape[0], HEADS * DV), BF16),
        in_specs=[smem] * 2 + [vmem] * 8,
        out_specs=vmem,
        scratch_shapes=[
            pltpu.VMEM((8, 4, 2, PACK, 128), BF16),
            pltpu.VMEM((2 * CN, SPACK, 128), BF16),
            pltpu.VMEM((2 * CN + 3, SPACK, 128), BF16),
            pltpu.VMEM((3, 2, PACK, 128), BF16),
            pltpu.VMEM((2, 1, 128), jnp.int32),
            pltpu.VMEM((CN, 2, 1, 128), jnp.int32),
            pltpu.VMEM((CN, 1, 128), jnp.int32),
            pltpu.SMEM((CN, 1, 128), jnp.int32),
            pltpu.VMEM((ROWS, 256), BF16),
            pltpu.VMEM((4, 144, CHUNK), F32),
            pltpu.VMEM((4, 8, CHUNK), F32),
            pltpu.VMEM((4, 128, CHUNK), F32),
            pltpu.VMEM((3, 4, 8, CHUNK), F32),
            pltpu.VMEM((1024, 256), BF16),
            pltpu.VMEM((144, 1024), BF16),
            pltpu.VMEM((1024, 128), BF16),
            pltpu.VMEM((2, 1024, CHUNK), F32),
            dma((ZN, 2)),
            dma((ZN, 2)),
            dma((ZN,)),
            dma((XN, ZN)),
            dma((8, 4, 2)),
            dma((CN,)),
            dma((CN,)),
            dma((2,)),
            dma((3,)),
            dma((3, 2)),
            dma((CN,)),
            dma((2,)),
            dma((CN,)),
            dma((CN,)),
            dma(()),
        ],
        compiler_params=pltpu.CompilerParams(
            collective_id=0, has_side_effects=True, vmem_limit_bytes=60 * 1024 * 1024
        ),
    )(
        cw,
        selections,
        selections,
        lengths,
        queries,
        sk,
        sv,
        pk.reshape(blocks, SBLK, DK),
        cv.reshape(blocks, SBLK, DV),
        jnp.transpose(gl, (0, 2, 1)),
    )


def solution(mesh):
    placed = (
        P(("ctx", "pb"), "ga"),
        P(("ctx", "pb"), "ga"),
        P(("ctx", "pb"), "ga"),
        P("ctx", "ga"),
        P("ctx", "ga"),
        P("ctx", None),
        P("ga", None),
        P(("ctx", "pb"), "ga", None),
        P(None, ("ctx", "pb"), "ga"),
    )
    return jax.shard_map(
        on_device, mesh=mesh, in_specs=placed, out_specs=P(("ctx", "pb"), "ga"), check_vma=False
    )
```

time: 152 us -> 131 us (0.86)
  the two profiles are of different devices: /device:TPU:89 before, /device:TPU:52 now
where the time goes in v2:
time: 131 us; the launch traced here: 130 us
  Pallas kernels  123 us (94%)
  local copies, waits for them, and re-layouts  7.28 us (6%)
    pallas_call x1, Pallas kernels, on_device(): pl.pallas_call(body, name='attend', out_shape=jax.ShapeDtypeStruct((queri...  123 us
    unnamed x3, local copies, waits for them, and re-layouts  7.28 us

profile of v2, /device:TPU:52, one launch (start us, length us, event | category | flops | bytes accessed | tf_op | source)
XLA Modules:
  0.0 130.3 jit_solution(6073707852137413752)
XLA Ops:
  0.0 1.5 %copy.11.sk = bf16[128,192]{1,0:T(8,128)(2,1)} copy(bf16[128,192]{0,1:T(8,128)(2,1)} %param.10) | data formatting | bytes 98304 | tf_op args[1]
  1.5 3.9 %copy.10 = bf16[4096,192]{1,0:T(8,128)(2,1)} copy(bf16[4096,192]{0,1:T(8,128)(2,1)} %param.12) | data formatting | bytes 3145728 | tf_op args[3]
  5.4 123.0 %attend.1 = bf16[128,2048]{1,0:T(8,128)(2,1)} custom-call(f32[1,32]{1,0:T(1,128)} %cw.1, s32[2,1,13]{2,1,0:T(1,128)} %sel.1, s32[2,1,13]{2,1,0:T(1,128)} %sel.1, s32[1,256]{1,0:T(1,128)} %lengths.1, bf16[128,3072]{1,0:T(8,128)(2,1)} %queries.1, bf16[128,192]{1,0:T(8,128)(2,1)} %copy.11.sk, bf16[128,128]{1,0:T(8,128)(2,1)} %sv.1, ...), custom_call_target="tpu_custom_call" | custom-call | tf_op jit(solution)/shard_map/attend/pallas_call | solution.py:606
  128.4 1.9 %copy.13 = bf16[128,2048]{1,0:T(8,128)(2,1)} copy(bf16[128,2048]{1,0:T(8,128)(2,1)} %attend.1) | data formatting | bytes 1048576

commit v3 on v2

--- a/solution.py
+++ b/solution.py
@@ -19,7 +19,8 @@
 SPACK = SBLK * 5 // 2
 ZSET = ((0, 1, 7, 2), (6, 3, 5, 4))
 ORDER = ((0, 0), (0, 1), (3, 0), (1, 0), (3, 1), (1, 1), (2, 0), (2, 1))
-PACE = (3, 3, 4, 4, 4, 4, 4, 5)
+PACE = (5, 5, 6, 6, 6, 3, 0, 0)
+ORIGIN = ((0, 0), (XN - 1, ZN - 1))
 ROWS = 2048
 CHUNK = 512
 MESH = pl.DeviceIdType.MESH
@@ -83,7 +84,9 @@
     w_send,
     wd_send,
     w_recv,
-    f_send,
+    fx_send,
+    fz_send,
+    fd_send,
     f_recv,
     q_send,
     q_recv,
@@ -286,31 +289,71 @@
         ref[at_index, 64:96, :] = a1.astype(BF16)
         ref[at_index, 96:160, :] = cv[number]
 
-    def first_fixed(i):
-        return remote(
-            recv.at[64], recv.at[64], f_send.at[i], f_recv.at[0], lax.rem(ctx + i, CN), p
+    def part(w, q):
+        if w:
+            return recv.at[65 + q]
+        return recv.at[64, pl.ds(pl.multiple_of(q * (SPACK // 2), 16), SPACK // 2)]
+
+    def to_f(w, dx, dz, sem):
+        return remote(part(w, p), part(w, p), sem, f_recv.at[w, p], at(dx, dz), p)
+
+    def to_fd(w):
+        return remote(part(w, p), part(w, p), fd_send.at[w], f_recv.at[w, p], ctx, other)
+
+    def got_f(w, q):
+        remote(part(w, q), part(w, q), fd_send.at[w], f_recv.at[w, q], ctx, other).wait_recv()
+
+    origin, hop, goes_up, goes_down = [], [], [], []
+    for ox, oz in ORIGIN:
+        away = lax.rem(z - oz + ZN, ZN)
+        origin.append((x == ox) & (z == oz))
+        hop.append(
+            jnp.where(
+                away == 0, jnp.where(x == ox, 0, 1), jnp.where(away <= 4, away + 1, 9 - away)
+            )
         )
-
-    def last_fixed(i):
-        return remote(
-            recv.at[pl.ds(65, 2)],
-            recv.at[pl.ds(65, 2)],
-            f_send.at[i],
-            f_recv.at[1],
-            lax.rem(ctx + i, CN),
-            p,
-        )
-
-    @pl.when(ctx == 0)
+        goes_up.append(away <= 3)
+        goes_down.append((away == 0) | (away >= 6))
+
+    def along_z(w, do):
+        @pl.when(goes_up[w])
+        def _():
+            do(to_f(w, 0, 1, fz_send.at[w, 0]))
+
+        @pl.when(goes_down[w])
+        def _():
+            do(to_f(w, 0, -1, fz_send.at[w, 1]))
+
+    def start(copy):
+        copy.start()
+
+    def sent(copy):
+        copy.wait_send()
+
+    def from_origin(w):
+        for k in range(1, XN):
+            to_f(w, k, 0, fx_send.at[w, k - 1]).start()
+        along_z(w, start)
+
+    @pl.when(origin[0])
     def _():
         store_block(recv, 64, 0)
-        start_all(first_fixed)
-
-    @pl.when(ctx == CN - 1)
+        from_origin(0)
+
+    @pl.when(origin[1])
     def _():
         store_block(recv, 65, SBLK - 2)
         store_block(recv, 66, SBLK - 1)
-        start_all(last_fixed)
+        from_origin(1)
+
+    def fixed(h):
+        for w in range(2):
+
+            @pl.when(hop[w] == h)
+            def _():
+                got_f(w, p)
+                to_fd(w).start()
+                along_z(w, start)
 
     lane = lax.broadcasted_iota(jnp.int32, (UNIT, 256), 1)
     for pair in range(HEADS // 2):
@@ -384,6 +427,8 @@
         return carry
 
     def listed(stage):
+        if not PACE[stage]:
+            return
         lax.fori_loop(1 + sum(PACE[:stage]), 1 + sum(PACE[: stage + 1]), fill, 0)
 
     listed(0)
@@ -402,10 +447,12 @@
             to_w(1).start()
 
     listed(1)
+    fixed(1)
 
     for zr in (2, 6):
         arrive(0, zr, p)
         spread_on(zr)
+    fixed(2)
 
     @pl.when(ctx >= 2)
     def _():
@@ -468,6 +515,8 @@
                 for zr in ZSET[far]:
                     arrive(2, zr, p)
                     to_d(2, zr).start()
+        if t < 3:
+            fixed(t + 3)
         if t < 6:
             listed(t + 2)
         for xr, zr in need:
@@ -509,13 +558,11 @@
 
     lax.fori_loop(1, CN, got_a, 0)
 
-    @pl.when(ctx != 0)
-    def _():
-        first_fixed(1).wait_recv()
-
-    @pl.when(ctx != CN - 1)
-    def _():
-        last_fixed(1).wait_recv()
+    for w in range(2):
+
+        @pl.when(hop[w] > 0)
+        def _():
+            got_f(w, other)
 
     ids = [sel_s[b, 0, n] for b in range(2) for n in range(13)]
     owner = [i // SBLK for i in ids]
@@ -589,13 +636,17 @@
     sent_all(to_q)
     sent_all(to_a)
 
-    @pl.when(ctx == 0)
-    def _():
-        sent_all(first_fixed)
-
-    @pl.when(ctx == CN - 1)
-    def _():
-        sent_all(last_fixed)
+    for w in range(2):
+        along_z(w, sent)
+
+        @pl.when(hop[w] > 0)
+        def _():
+            to_fd(w).wait_send()
+
+        @pl.when(origin[w])
+        def _():
+            for k in range(1, XN):
+                to_f(w, k, 0, fx_send.at[w, k - 1]).wait_send()
 
 
 def on_device(queries, sk, sv, pk, cv, lengths, cw, selections, gl):
@@ -637,8 +688,10 @@
             dma((2,)),
             dma((3,)),
             dma((3, 2)),
-            dma((CN,)),
+            dma((2, 3)),
+            dma((2, 2)),
             dma((2,)),
+            dma((2, 2)),
             dma((CN,)),
             dma((CN,)),
             dma(()),

time: 131 us -> 104 us (0.79)
  the two profiles are of different devices: /device:TPU:52 before, /device:TPU:1 now
where the time goes in v3:
time: 104 us; the launch traced here: 102 us
  Pallas kernels  94.5 us (91%)
  local copies, waits for them, and re-layouts  7.28 us (7%)
    pallas_call x1, Pallas kernels, on_device(): pl.pallas_call(body, name='attend', out_shape=jax.ShapeDtypeStruct((queri...  94.5 us
    unnamed x3, local copies, waits for them, and re-layouts  7.28 us

profile of v3, /device:TPU:1, one launch (start us, length us, event | category | flops | bytes accessed | tf_op | source)
XLA Modules:
  0.0 101.8 jit_solution(2923873986914242919)
XLA Ops:
  0.0 1.5 %copy.11.sk = bf16[128,192]{1,0:T(8,128)(2,1)} copy(bf16[128,192]{0,1:T(8,128)(2,1)} %param.10) | data formatting | bytes 98304 | tf_op args[1]
  1.5 3.9 %copy.10 = bf16[4096,192]{1,0:T(8,128)(2,1)} copy(bf16[4096,192]{0,1:T(8,128)(2,1)} %param.12) | data formatting | bytes 3145728 | tf_op args[3]
  5.4 94.5 %attend.1 = bf16[128,2048]{1,0:T(8,128)(2,1)} custom-call(f32[1,32]{1,0:T(1,128)} %cw.1, s32[2,1,13]{2,1,0:T(1,128)} %sel.1, s32[2,1,13]{2,1,0:T(1,128)} %sel.1, s32[1,256]{1,0:T(1,128)} %lengths.1, bf16[128,3072]{1,0:T(8,128)(2,1)} %queries.1, bf16[128,192]{1,0:T(8,128)(2,1)} %copy.11.sk, bf16[128,128]{1,0:T(8,128)(2,1)} %sv.1, ...), custom_call_target="tpu_custom_call" | custom-call | tf_op jit(solution)/shard_map/attend/pallas_call | solution.py:657
  99.9 1.9 %copy.13 = bf16[128,2048]{1,0:T(8,128)(2,1)} copy(bf16[128,2048]{1,0:T(8,128)(2,1)} %attend.1) | data formatting | bytes 1048576

commit v4 on v3

--- a/solution.py
+++ b/solution.py
@@ -19,7 +19,7 @@
 SPACK = SBLK * 5 // 2
 ZSET = ((0, 1, 7, 2), (6, 3, 5, 4))
 ORDER = ((0, 0), (0, 1), (3, 0), (1, 0), (3, 1), (1, 1), (2, 0), (2, 1))
-PACE = (5, 5, 6, 6, 6, 3, 0, 0)
+PACE = (6, 9, 10, 6, 0, 0, 0, 0)
 ORIGIN = ((0, 0), (XN - 1, ZN - 1))
 ROWS = 2048
 CHUNK = 512
@@ -53,10 +53,11 @@
     queries,
     sk,
     sv,
-    ck,
+    ckt,
     cv,
     gl,
     out,
+    ck,
     gat,
     send,
     recv,
@@ -128,7 +129,7 @@
     reqs[0] = jnp.full((2, 1, 128), -1, jnp.int32)
     for b in range(2):
         reqs[0, b, :, 0:13] = sel[b]
-    k0, k1 = pack_keys(sk[...].astype(F32))
+    k0, k1 = pack_keys(sk[...].astype(F32).T)
     win[0, p, 0:128, :] = k0.astype(BF16)
     win[0, p, 128:192, :] = k1.astype(BF16)
     win[0, p, 192:320, :] = sv[...].astype(F32).T.astype(BF16)
@@ -144,7 +145,7 @@
     starts = jnp.sum(jnp.where(j_at < b_at, n_row, 0.0), axis=1, keepdims=True)
     counts = jnp.sum(jnp.where(j_at == b_at, n_row, 0.0), axis=1, keepdims=True)
     spread = 1.0 / jnp.sqrt(counts)
-    span = ck.shape[0] * SBLK
+    span = ckt.shape[1]
     step = 512
     total_k = jnp.zeros((UNIT, DK), F32)
     total_v = jnp.zeros((UNIT, DV), F32)
@@ -157,7 +158,8 @@
         for i in range(32):
             weight = jnp.where(off == float(i), cw[0, i], weight)
         matrix = jnp.where(member, weight * spread, 0.0).astype(BF16)
-        rows = ck[t // SBLK : (t + step) // SBLK].reshape(step, DK)
+        rows = ckt[:, t : t + step].T
+        ck[t // SBLK : (t + step) // SBLK] = rows.reshape(step // SBLK, SBLK, DK)
         vals = cv[t // SBLK : (t + step) // SBLK].reshape(step, DV)
         total_k += jnp.dot(matrix, rows, preferred_element_type=F32)
         total_v += jnp.dot(matrix, vals, preferred_element_type=F32)
@@ -661,6 +663,7 @@
         in_specs=[smem] * 2 + [vmem] * 8,
         out_specs=vmem,
         scratch_shapes=[
+            pltpu.VMEM((blocks, SBLK, DK), BF16),
             pltpu.VMEM((8, 4, 2, PACK, 128), BF16),
             pltpu.VMEM((2 * CN, SPACK, 128), BF16),
             pltpu.VMEM((2 * CN + 3, SPACK, 128), BF16),
@@ -705,9 +708,9 @@
         selections,
         lengths,
         queries,
-        sk,
+        sk.T,
         sv,
-        pk.reshape(blocks, SBLK, DK),
+        pk.T,
         cv.reshape(blocks, SBLK, DV),
         jnp.transpose(gl, (0, 2, 1)),
     )

time: 104 us -> 102 us (0.981); the launches traced: 102 us -> 102 us
  Pallas kernels: 94.5 us -> 100 us
  local copies, waits for them, and re-layouts: 7.28 us -> 1.88 us
    pallas_call x1, Pallas kernels: 94.5 us -> 100 us  [on_device(): pl.pallas_call(body, name='attend', out_shape=jax.ShapeDtypeStruct((queri...]
    unnamed x3 -> x1, local copies, waits for them, and re-layouts: 7.28 us -> 1.88 us
where the time goes in v4:
time: 102 us
  Pallas kernels  100 us (98%)
  local copies, waits for them, and re-layouts  1.88 us (2%)
    pallas_call x1, Pallas kernels, on_device(): pl.pallas_call(body, name='attend', out_shape=jax.ShapeDtypeStruct((queri...  100 us

profile of v4, /device:TPU:1, one launch (start us, length us, event | category | flops | bytes accessed | tf_op | source)
XLA Modules:
  0.0 102.1 jit_solution(8808223969364726638)
XLA Ops:
  0.0 100.2 %attend.1 = bf16[128,2048]{1,0:T(8,128)(2,1)} custom-call(f32[1,32]{1,0:T(1,128)} %cw.1, s32[2,1,13]{2,1,0:T(1,128)} %sel.1, s32[2,1,13]{2,1,0:T(1,128)} %sel.1, s32[1,256]{1,0:T(1,128)} %lengths.1, bf16[128,3072]{1,0:T(8,128)(2,1)} %queries.1, bf16[192,128]{1,0:T(8,128)(2,1)} %bitcast.6, bf16[128,128]{1,0:T(8,128)(2,1)} %sv.1, bf16[192,4096]{1,0:T(8,128)(2,1)} %bitcast.4, ...), custom_call_target="tpu_custom_call" | custom-call | tf_op jit(solution)/shard_map/attend/pallas_call | solution.py:659
  100.2 1.9 %copy.11 = bf16[128,2048]{1,0:T(8,128)(2,1)} copy(bf16[128,2048]{1,0:T(8,128)(2,1)} %attend.1) | data formatting | bytes 1048576

commit v5 on v4

--- a/solution.py
+++ b/solution.py
@@ -19,7 +19,7 @@
 SPACK = SBLK * 5 // 2
 ZSET = ((0, 1, 7, 2), (6, 3, 5, 4))
 ORDER = ((0, 0), (0, 1), (3, 0), (1, 0), (3, 1), (1, 1), (2, 0), (2, 1))
-PACE = (6, 9, 10, 6, 0, 0, 0, 0)
+PACE = (6, 5, 6, 6, 5, 3, 0, 0)
 ORIGIN = ((0, 0), (XN - 1, ZN - 1))
 ROWS = 2048
 CHUNK = 512
@@ -139,6 +139,33 @@
         def _():
             win[k] = jnp.zeros((2, PACK, 128), BF16)
 
+    pl.semaphore_wait(barrier, 2 * CN - 1)
+
+    def to_q(i):
+        dx, dz = i // ZN, lax.rem(i, ZN)
+        back = lax.rem(XN - dx, XN) * ZN + lax.rem(ZN - dz, ZN)
+        return remote(mine, reqs.at[back], q_send.at[i], q_recv.at[back], at(dx, dz), p)
+
+    def got_q(i, carry):
+        remote(mine, reqs.at[i], q_send.at[i], q_recv.at[i], ctx, other).wait_recv()
+        return carry
+
+    def start_all(make):
+        def one(i, carry):
+            make(i).start()
+            return carry
+
+        lax.fori_loop(1, CN, one, 0)
+
+    def sent_all(make):
+        def one(i, carry):
+            make(i).wait_send()
+            return carry
+
+        lax.fori_loop(1, CN, one, 0)
+
+    start_all(to_q)
+
     b_at = p * UNIT + lax.broadcasted_iota(jnp.int32, (UNIT, 256), 0)
     j_at = lax.broadcasted_iota(jnp.int32, (UNIT, 256), 1)
     n_row = jnp.broadcast_to(lengths[...], (UNIT, 256)).astype(F32)
@@ -168,33 +195,6 @@
     gat[0, 0, p, 128:192, :] = k1.astype(BF16)
     gat[0, 0, p, 192:320, :] = total_v.T.astype(BF16)
 
-    pl.semaphore_wait(barrier, 2 * CN - 1)
-
-    def to_q(i):
-        dx, dz = i // ZN, lax.rem(i, ZN)
-        back = lax.rem(XN - dx, XN) * ZN + lax.rem(ZN - dz, ZN)
-        return remote(mine, reqs.at[back], q_send.at[i], q_recv.at[back], at(dx, dz), p)
-
-    def got_q(i, carry):
-        remote(mine, reqs.at[i], q_send.at[i], q_recv.at[i], ctx, other).wait_recv()
-        return carry
-
-    def start_all(make):
-        def one(i, carry):
-            make(i).start()
-            return carry
-
-        lax.fori_loop(1, CN, one, 0)
-
-    def sent_all(make):
-        def one(i, carry):
-            make(i).wait_send()
-            return carry
-
-        lax.fori_loop(1, CN, one, 0)
-
-    start_all(to_q)
-
     def g_at(xr, zr, q):
         t, n = slot(xr, zr)
         return gat.at[t, n, q]
@@ -356,16 +356,6 @@
                 got_f(w, p)
                 to_fd(w).start()
                 along_z(w, start)
-
-    lane = lax.broadcasted_iota(jnp.int32, (UNIT, 256), 1)
-    for pair in range(HEADS // 2):
-        both = queries[:, pair * 384 : (pair + 1) * 384].astype(F32)
-        first = jnp.where(lane < DK, both[:, 0:256], 0.0).astype(BF16)
-        second = jnp.where(lane < DK, pltpu.roll(both[:, 128:384], 192, 1), 0.0).astype(BF16)
-        for h, rows in ((2 * pair, first), (2 * pair + 1, second)):
-            for b in range(2):
-                base = b * 1024 + h * 64
-                qs[base : base + 64, :] = rows[b * 64 : b * 64 + 64]
 
     lfn = pltpu.make_async_copy(offs, asked, l_sem)
     lax.fori_loop(1, CN, got_q, 0)
@@ -434,6 +424,17 @@
         lax.fori_loop(1 + sum(PACE[:stage]), 1 + sum(PACE[: stage + 1]), fill, 0)
 
     listed(0)
+
+    lane = lax.broadcasted_iota(jnp.int32, (UNIT, 256), 1)
+    for pair in range(HEADS // 2):
+        both = queries[:, pair * 384 : (pair + 1) * 384].astype(F32)
+        first = jnp.where(lane < DK, both[:, 0:256], 0.0).astype(BF16)
+        second = jnp.where(lane < DK, pltpu.roll(both[:, 128:384], 192, 1), 0.0).astype(BF16)
+        for h, rows in ((2 * pair, first), (2 * pair + 1, second)):
+            for b in range(2):
+                base = b * 1024 + h * 64
+                qs[base : base + 64, :] = rows[b * 64 : b * 64 + 64]
+
 
     for zr in (1, 7):
         arrive(0, zr, p)

time: 102 us -> 99.1 us (0.972); the launches traced: 102 us -> 97.2 us
  Pallas kernels: 100 us -> 95.3 us
    pallas_call x1, Pallas kernels: 100 us -> 95.3 us  [on_device(): pl.pallas_call(body, name='attend', out_shape=jax.ShapeDtypeStruct((queri...]
where the time goes in v5:
time: 99.1 us; the launch traced here: 97.2 us
  Pallas kernels  95.3 us (96%)
  local copies, waits for them, and re-layouts  1.88 us (2%)
    pallas_call x1, Pallas kernels, on_device(): pl.pallas_call(body, name='attend', out_shape=jax.ShapeDtypeStruct((queri...  95.3 us

profile of v5, /device:TPU:1, one launch (start us, length us, event | category | flops | bytes accessed | tf_op | source)
XLA Modules:
  0.0 97.2 jit_solution(5600375783594092455)
XLA Ops:
  0.0 95.3 %attend.1 = bf16[128,2048]{1,0:T(8,128)(2,1)} custom-call(f32[1,32]{1,0:T(1,128)} %cw.1, s32[2,1,13]{2,1,0:T(1,128)} %sel.1, s32[2,1,13]{2,1,0:T(1,128)} %sel.1, s32[1,256]{1,0:T(1,128)} %lengths.1, bf16[128,3072]{1,0:T(8,128)(2,1)} %queries.1, bf16[192,128]{1,0:T(8,128)(2,1)} %bitcast.6, bf16[128,128]{1,0:T(8,128)(2,1)} %sv.1, bf16[192,4096]{1,0:T(8,128)(2,1)} %bitcast.4, ...), custom_call_target="tpu_custom_call" | custom-call | tf_op jit(solution)/shard_map/attend/pallas_call | solution.py:660
  95.4 1.9 %copy.11 = bf16[128,2048]{1,0:T(8,128)(2,1)} copy(bf16[128,2048]{1,0:T(8,128)(2,1)} %attend.1) | data formatting | bytes 1048576
